TPU v7x, 256 devices: a whole 4x4x8 slice. The times are simulated.
256 devices in a mesh: vis: 32 (over x, z), tile: 8 (over y, core).
Axes of the slice: x: 4, y: 4, z: 8, core: 2. Of those that a mesh axis runs over, the one named last changes fastest.
Arguments:
- spectra: bfloat16 [64, 2048], P(None, ('vis', 'tile')), may hold values from -0.1875 to 0.1875
- positions: int32 [2, 2048], P(None, ('vis', 'tile')), may hold values from 0 to 8191
- observed: bfloat16 [262144, 128], P(('vis', 'tile')), may hold values from -6 to 6
- cells: int32 [2, 262144], P(None, ('vis', 'tile')), may hold values from 0 to 8184, as said below
- fractions: float32 [2, 262144], P(None, ('vis', 'tile')), may hold values from 0 to 1
- bucket_counts: int32 [256, 8], P(('vis', 'tile')), may hold values from 0 to 512, as said below
- chan_weights: float32 [64], replicated, may hold values from 0.04 to 0.32
Outputs:
- residual_vis: bfloat16 [262144, 128], P(('vis', 'tile'))
- residual_grid: float32 [128, 2, 8192], P('vis', None, 'tile')
Inputs may be any that keep to these rules, and one draw needn't show every extreme that they name: cells[0, r] is the first uv column and cells[1, r] the first uv row of row r's 8 x 8 kernel window, with cells[1, r] <= 120. The rows of each device are ordered by tile: for device d and tile t, the bucket_counts[d, t] rows that start after the first sum of bucket_counts[d, 0:t] rows have cells[0] between t * 1024 and (t + 1) * 1024 - 8; rows after a device's total are unused. `bucket_counts`: each device's counts sum to at most 1024. For every index of vis, one tile receives exactly 512 rows from every device with that vis index; which tile is drawn.
All inputs are finite; a program needn't handle non-finite values.
Results may differ from a plain program's by a relative error of at most 0.008.
Values may be sent and summed in bfloat16 or wider, within the bound.
No kernel may reach another device: no remote copies, remote signals or barrier semaphores. Data moves between devices by JAX's collectives and lax.ppermute only.
A program may use at most 64 MiB of HBM per device.

v0:
```python
import math

import jax
import jax.numpy as jnp
from jax import lax
from jax.sharding import Mesh
from jax.sharding import PartitionSpec as P

GRID = 8192
BAND = 128
TAPS = 8
TILE = ("tile_0", "tile_1")
VIS = ("vis_0", "vis_1")
VIS_TILE = ("vis_0", "vis_1", "tile_0", "tile_1")


def whole_of(array, axes, dim):
    result = array
    for number in range(len(axes) - 1, -1, -1):
        result = lax.all_gather(result, axes[number], axis=dim, tiled=True)
    return result


def side_by_side(arrays, axis, split_dim, concat_dim, along):
    widths = [math.prod(a.shape[along:]) for a in arrays]
    both = jnp.concatenate(
        [a.reshape(*a.shape[:along], w) for a, w in zip(arrays, widths)], axis=along
    )
    result = lax.all_to_all(both, axis, split_axis=split_dim, concat_axis=concat_dim, tiled=True)
    parts = jnp.split(result, [sum(widths[:k]) for k in range(1, len(widths))], axis=along)
    return tuple(
        (b.reshape(*result.shape[:along], *a.shape[along:]) for a, b in zip(arrays, parts))
    )


def predict_piece(running, shard_part, first_col, first_row, col_frac, row_frac):
    spec_piece, pos_piece = shard_part
    col_pixel = pos_piece[0]
    row_pixel = pos_piece[1]
    turn_count = jnp.mod(
        (first_col + 3)[:, None] * col_pixel[None, :]
        + (first_row + 3)[:, None] * row_pixel[None, :],
        GRID,
    )
    phase_turns = (
        turn_count.astype(jnp.float32)
        + col_frac[:, None] * col_pixel.astype(jnp.float32)[None, :]
        + row_frac[:, None] * row_pixel.astype(jnp.float32)[None, :]
    )
    angles = phase_turns * (2.0 * math.pi / GRID)
    cosine = jnp.cos(angles).astype(jnp.bfloat16)
    sine_table = jnp.sin(angles).astype(jnp.bfloat16)
    contract_dims = (((1,), (1,)), ((), ()))
    real_part = lax.dot_general(
        cosine, spec_piece, contract_dims, preferred_element_type=jnp.float32
    )
    imag_part = lax.dot_general(
        sine_table, spec_piece, contract_dims, preferred_element_type=jnp.float32
    )
    return (real_part, running[1] - imag_part)


def kernel_weights(offsets):
    taps_float = jnp.arange(TAPS, dtype=jnp.int32).astype(jnp.float32)
    shifted = taps_float[None, :] - 3.0 - offsets[:, None]
    return jnp.exp(-0.5 * (shifted * shifted))


def place_taps(offset, tap_table):
    placed = jnp.zeros(offset.shape, jnp.float32)
    for tap_number in range(TAPS):
        placed = jnp.where(offset == tap_number, tap_table[:, tap_number : tap_number + 1], placed)
    return placed


def spread_rows(first_col, col_frac, col_base, tile_width):
    offset = jnp.arange(tile_width, dtype=jnp.int32)[None, :] - (first_col - col_base)[:, None]
    return place_taps(offset, kernel_weights(col_frac)).astype(jnp.bfloat16)


def left_rows(values, first_row, row_frac, band_count):
    offset = jnp.arange(band_count, dtype=jnp.int32)[None, :] - first_row[:, None]
    weight = place_taps(offset, kernel_weights(row_frac))
    return (values[:, :, None] * weight[None, :, :]).astype(jnp.bfloat16)


def accumulate(spread, values, first_row, row_frac, group_total, band_count):
    slot_total = spread.shape[0]
    tile_width = spread.shape[1]
    group_size = slot_total // group_total
    block_rows = min(256, group_size)
    per_group = group_size // block_rows
    block_total = slot_total // block_rows
    spread_blocks = spread.reshape(block_total, block_rows, tile_width)
    value_blocks = values.reshape(2, block_total, block_rows).transpose(1, 0, 2)
    row_blocks = first_row.reshape(block_total, block_rows)
    frac_blocks = row_frac.reshape(block_total, block_rows)
    group_of = jnp.arange(block_total, dtype=jnp.int32) // per_group

    def block_term(block_data):
        left_table = left_rows(block_data[1], block_data[2], block_data[3], band_count)
        return jnp.einsum(
            "cbv,bu->vcu", left_table, block_data[0], preferred_element_type=jnp.float32
        )

    def scan_step(totals, block_data):
        totals = totals + block_term(block_data)
        return (totals, None)

    start_totals = jnp.zeros((band_count, 2, tile_width), jnp.float32)
    finished, unused = lax.scan(
        scan_step, start_totals, (spread_blocks, value_blocks, row_blocks, frac_blocks, group_of)
    )
    return finished


def on_device(spectra, positions, observed, cells, fractions, bucket_counts, chan_weights):
    row_count = observed.shape[0]
    channels = observed.shape[1] // 2
    tile_count = lax.axis_size(TILE)
    tile_width = GRID // tile_count
    slot_size = row_count // 2
    band_rows = BAND // lax.axis_size(VIS)
    first_col = cells[0]
    first_row = cells[1]
    col_frac = fractions[0]
    row_frac = fractions[1]
    bucket_sizes = bucket_counts[0]
    zeros_init = jnp.zeros((row_count, channels), jnp.float32)
    real_part, imag_part = predict_piece(
        (zeros_init, zeros_init),
        (
            whole_of(spectra, ("tile_1", "tile_0", "vis_1", "vis_0"), 1),
            whole_of(positions, ("tile_1", "tile_0", "vis_1", "vis_0"), 1),
        ),
        first_col,
        first_row,
        col_frac,
        row_frac,
    )
    predicted = jnp.concatenate([real_part, imag_part], axis=1)
    row_live = jnp.arange(row_count, dtype=jnp.int32) < jnp.sum(bucket_sizes)
    residual = jnp.where(row_live[:, None], observed.astype(jnp.float32) - predicted, 0.0).astype(
        jnp.bfloat16
    )
    widened = residual.astype(jnp.float32)
    value_real = jnp.sum(widened[:, :channels] * chan_weights[None, :], axis=1)
    value_imag = jnp.sum(widened[:, channels:] * chan_weights[None, :], axis=1)
    bucket_start = jnp.cumsum(bucket_sizes) - bucket_sizes
    slot_index = bucket_start[:, None] + jnp.arange(slot_size, dtype=jnp.int32)[None, :]
    slot_live = jnp.arange(slot_size, dtype=jnp.int32)[None, :] < bucket_sizes[:, None]
    float_rows = jnp.pad(
        jnp.stack([value_real, value_imag, col_frac, row_frac]), ((0, 0), (0, slot_size))
    )
    cell_rows = jnp.pad(cells, ((0, 0), (0, slot_size)))
    gathered = jnp.take(float_rows, slot_index, axis=1).transpose(1, 0, 2)
    packed_values = jnp.concatenate(
        [jnp.where(slot_live[:, None, :], gathered[:, 0:2], 0.0), gathered[:, 2:]], axis=1
    )
    packed_cells = jnp.take(cell_rows, slot_index, axis=1).transpose(1, 0, 2)
    slot_total = tile_count * slot_size
    got_values, got_cells, got_sizes = (
        lax.all_to_all(packed_values, TILE, split_axis=0, concat_axis=0, tiled=True),
        *side_by_side((packed_cells, bucket_sizes[:, None]), TILE, 0, 0, 1),
    )
    values = got_values[:, 0:2].transpose(1, 0, 2).reshape(2, slot_total)
    spread = spread_rows(
        got_cells[:, 0].reshape(slot_total),
        got_values[:, 2].reshape(slot_total),
        lax.axis_index(TILE) * tile_width,
        tile_width,
    )
    owner_rows = got_cells[:, 1].reshape(slot_total)
    owner_frac = got_values[:, 3].reshape(slot_total)
    grid_share = lax.psum_scatter(
        accumulate(
            spread, values, owner_rows, owner_frac, tile_count, band_rows * lax.axis_size(VIS)
        ),
        VIS,
        scatter_dimension=0,
        tiled=True,
    )
    return (residual, grid_share)


def solution(mesh):
    torus = Mesh(mesh.devices.reshape(4, 8, 4, 2), ("vis_0", "vis_1", "tile_0", "tile_1"))
    return jax.shard_map(
        on_device,
        mesh=torus,
        in_specs=(
            P(None, VIS_TILE),
            P(None, VIS_TILE),
            P(VIS_TILE, None),
            P(None, VIS_TILE),
            P(None, VIS_TILE),
            P(VIS_TILE, None),
            P(),
        ),
        out_specs=(P(VIS_TILE, None), P(VIS, None, TILE)),
        check_vma=False,
    )
```

profile of v0, /device:TPU:32, one launch (start us, length us, event | category | flops | bytes accessed | tf_op | source)
XLA Modules:
  0.0 424.6 jit_solution(6332408301654448321)
XLA Ops:
  7.2 0.9 reduce-window.8
  8.1 0.7 bitcast_subtract_fusion
  8.9 0.7 copy.34
  9.6 0.9 copy.32
  10.6 10.8 %gather_fusion = s32[4096,2]{1,0:T(8,128)S(1)} fusion(s32[2,1536]{0,1:T(8,128)S(1)} %pad.8, s32[4096]{0:T(1024)S(1)} %broadcast_clamp_fusion), kind=kCustom, calls=%fused_computation | custom fusion | bytes 81920 | tf_op jit(solution)/shard_map/jit(_take)/gather | solution.py:160
  22.1 0.7 copy.35
  22.7 4.5 %all-to-all-start = ((s32[8,1,1025]{2,1,0:T(1,128)}), s32[8,1,1025]{2,1,0:T(1,128)S(1)}, u32[]{:S(2)}, u32[]{:S(2)}) async-start(s32[8,1,1025]{2,1,0:T(1,128)} %copy.35), calls=%async_computation | async-start | bytes 73728 | tf_op jit(solution)/shard_map/all_to_all | solution.py:29
  27.2 0.8 slice_add_fusion.1
  28.0 10.0 %all-gather = s32[4,8,2]{1,2,0:T(2,128)S(1)} all-gather(s32[1,8,2]{1,2,0:T(2,128)} %bitcast.144), channel_id=1, replica_groups=mesh['vis_0'=4,'vis_1'=8,'tile_0'=4,'tile_1'=2] {'vis_0'}, dimensions={0}, use_global_device_ids=true | all-gather | bytes 320 | tf_op jit(solution)/shard_map/all_gather | solution.py:20
  38.1 17.0 %all-gather.1 = s32[8,32,2]{1,2,0:T(2,128)S(1)} all-gather(s32[1,32,2]{1,2,0:T(2,128)S(1)} %reshape.407), channel_id=1, replica_groups=mesh['vis_0'=4,'vis_1'=8,'tile_0'=4,'tile_1'=2] {'vis_1'}, dimensions={0}, use_global_device_ids=true | all-gather | bytes 2304 | tf_op jit(solution)/shard_map/all_gather | solution.py:20
  55.2 11.7 %all_gather.26 = s32[2,1024]{1,0:T(2,128)S(1)} all-gather(s32[2,256]{1,0:T(2,128)S(1)} %bitcast.140), channel_id=1, replica_groups=mesh['vis_0'=4,'vis_1'=8,'tile_0'=4,'tile_1'=2] {'tile_0'}, dimensions={1}, use_global_device_ids=true | all-gather | bytes 10240 | tf_op jit(solution)/shard_map/all_gather | solution.py:20
  66.8 1.8 all_gather.27
  68.6 0.8 fusion.53
  69.4 35.1 %cosine_convert_fusion.4 = bf16[1024,2048]{1,0:T(8,128)(2,1)} fusion(f32[2048]{0:T(1024)S(1)} %bitcast.123, f32[1024]{0:T(1024)S(1)} %bitcast.136, f32[2048]{0:T(1024)S(1)} %bitcast.121, f32[1024]{0:T(1024)S(1)} %bitcast.134, s32[2048]{0:T(1024)S(1)} %bitcast.125, s32[1024]{0:T(1024)S(1)} %bitcast.132, s32[2048]{0:T(1024)S(1)} %bitcast.119, ...), kind=kLoop, calls=%fused_computation.45.clone.clone.1 | loop fusion | flops 44040192 | bytes 4243456 | tf_op jit(solution)/shard_map/dot_general | solution.py:54
  104.5 35.5 %sine_convert_fusion.6 = bf16[1024,2048]{1,0:T(8,128)(2,1)} fusion(f32[2048]{0:T(1024)S(1)} %bitcast.124, f32[1024]{0:T(1024)S(1)} %bitcast.137, f32[2048]{0:T(1024)S(1)} %bitcast.122, f32[1024]{0:T(1024)S(1)} %bitcast.135, s32[2048]{0:T(1024)S(1)} %bitcast.126, s32[1024]{0:T(1024)S(1)} %bitcast.133, s32[2048]{0:T(1024)S(1)} %bitcast.120, ...), kind=kLoop, calls=%fused_computation.44.clone.clone.clone.clone.1 | loop fusion | flops 44040192 | bytes 4243456 | tf_op jit(solution)/shard_map/dot_general | solution.py:57
  140.6 10.4 %all_gather.28 = bf16[64,32]{0,1:T(8,128)(2,1)S(1)} all-gather(bf16[64,8]{0,1:T(8,128)(2,1)S(1)} %copy-done.2), channel_id=1, replica_groups=mesh['vis_0'=4,'vis_1'=8,'tile_0'=4,'tile_1'=2] {'vis_0'}, dimensions={1}, use_global_device_ids=true | all-gather | bytes 5120 | tf_op jit(solution)/shard_map/all_gather | solution.py:20
  151.0 23.6 %all_gather.29 = bf16[64,256]{0,1:T(8,128)(2,1)S(1)} all-gather(bf16[64,32]{0,1:T(8,128)(2,1)S(1)} %all_gather.28), channel_id=1, replica_groups=mesh['vis_0'=4,'vis_1'=8,'tile_0'=4,'tile_1'=2] {'vis_1'}, dimensions={1}, use_global_device_ids=true | all-gather | bytes 36864 | tf_op jit(solution)/shard_map/all_gather | solution.py:20
  174.6 12.2 %all_gather.30 = bf16[64,1024]{0,1:T(8,128)(2,1)S(1)} all-gather(bf16[64,256]{0,1:T(8,128)(2,1)S(1)} %all_gather.29), channel_id=1, replica_groups=mesh['vis_0'=4,'vis_1'=8,'tile_0'=4,'tile_1'=2] {'tile_0'}, dimensions={1}, use_global_device_ids=true | all-gather | bytes 163840 | tf_op jit(solution)/shard_map/all_gather | solution.py:20
  186.9 2.4 all_gather.31
  189.2 3.6 fusion.27
  192.8 3.6 fusion.31
  196.6 0.7 iota_compare_fusion.1
  197.8 10.8 %gather_fusion.1 = f32[4096,4]{1,0:T(8,128)S(1)} fusion(f32[4,1536]{0,1:T(8,128)S(1)} %pad.9, s32[4096]{0:T(1024)S(1)} %broadcast_clamp_fusion), kind=kCustom, calls=%fused_computation.1 | custom fusion | bytes 147456 | tf_op jit(solution)/shard_map/jit(_take)/gather | solution.py:156
  209.3 0.7 pad_maximum_fusion
  210.0 3.4 all-to-all-start.1
  213.5 5.4 %all-to-all-done.1 = f32[8,4,512]{2,1,0:T(4,128)S(1)} async-done(((f32[8,4,512]{2,1,0:T(4,128)}), f32[8,4,512]{2,1,0:T(4,128)S(1)}, u32[]{:S(2)}, u32[]{:S(2)}) %all-to-all-start.1) | async-done | bytes 65568 | tf_op jit(solution)/shard_map/all_to_all | solution.py:163
  219.6 13.5 %select_convert_fusion = bf16[16,256,1024]{1,2,0:T(8,128)(2,1)} fusion(bf16[16,256]{1,0:T(8,128)(2,1)S(1)} %broadcast_in_dim.215, bf16[16,256]{1,0:T(8,128)(2,1)S(1)} %broadcast_in_dim.213, bf16[16,256]{1,0:T(8,128)(2,1)S(1)} %broadcast_in_dim.211, bf16[16,256]{1,0:T(8,128)(2,1)S(1)} %broadcast_in_dim.209, bf16[16,256]{1,0:T(8,128)(2,1)S(1)} %broadcast_in_dim.207, ...), kind=kLoop, calls=%fused_computation.26 | loop fusion | flops 71303168 | bytes 8470528 | tf_op jit(solution)/shard_map/convert_element_type | solution.py:78
  233.1 34.4 %while.13 = (s32[]{:T(128)}, f32[128,2,1024]{0,2,1:T(8,128)S(1)}, bf16[16,256,1024]{1,2,0:T(8,128)(2,1)}, f32[16,2,256]{2,0,1:T(8,128)S(1)}, s32[16,256]{1,0:T(8...) while((s32[]{:T(128)}, f32[128,2,1024]{0,2,1:T(8,128)S(1)}, ...), condition=%wide.region_5.6_spmd.clone, body=%wide.region_4.5_spmd.clone.sunk | while | flops 135436304 | bytes 2933419 | solution.py:111
  233.6 1.6 fusion.65
  235.8 1.6 fusion.65
  237.9 1.6 fusion.65
  240.1 1.6 fusion.65
  242.2 1.6 fusion.65
  244.4 1.6 fusion.65
  246.5 1.6 fusion.65
  248.7 1.6 fusion.65
  250.8 1.6 fusion.65
  253.0 1.6 fusion.65
  255.1 1.6 fusion.65
  257.3 1.6 fusion.65
  259.4 1.6 fusion.65
  261.6 1.6 fusion.65
  263.7 1.6 fusion.65
  265.9 1.6 fusion.65
  267.5 1.3 copy.40
  268.8 0.8 copy.41
  270.9 145.5 %all-reduce.5.cloned.1.call-done = f32[128,2,1024]{2,1,0:T(2,128)} async-done(((f32[128,2,1024]{2,1,0:T(2,128)}), f32[128,2,1024]{2,1,0:T(2,128)}) %all-reduce.5.cloned.1.call-update) | async-done | bytes 1048592
  416.4 1.4 constant_dynamic-slice_fusion.3
  (191 shorter events, 12.4 us)
Async XLA Ops:
  7.2 132.8 %copy-start.3 = (s32[1,8]{1,0:T(1,128)S(1)}, s32[1,8]{1,0:T(1,128)}, u32[]{:S(2)}) copy-start(s32[1,8]{1,0:T(1,128)} %param.14) | copy-start | bytes 100
  7.2 133.4 %copy-start.2 = (bf16[64,8]{0,1:T(8,128)(2,1)S(1)}, bf16[64,8]{0,1:T(8,128)(2,1)}, u32[]{:S(2)}) copy-start(bf16[64,8]{0,1:T(8,128)(2,1)} %param.9) | copy-start | bytes 3076
  22.7 187.3 %all-to-all-start = ((s32[8,1,1025]{2,1,0:T(1,128)}), s32[8,1,1025]{2,1,0:T(1,128)S(1)}, u32[]{:S(2)}, u32[]{:S(2)}) async-start(s32[8,1,1025]{2,1,0:T(1,128)} %copy.35), calls=%async_computation | async-start | bytes 73728 | tf_op jit(solution)/shard_map/all_to_all | solution.py:29
  104.5 91.9 %copy-start = (bf16[1024,128]{1,0:T(8,128)(2,1)S(1)}, bf16[1024,128]{1,0:T(8,128)(2,1)}, u32[]{:S(2)}) copy-start(bf16[1024,128]{1,0:T(8,128)(2,1)} %param.11) | copy-start | bytes 786436
  104.5 92.8 %copy-start.4 = (f32[64]{0:T(128)S(1)}, f32[64]{0:T(128)}, u32[]{:S(2)}) copy-start(f32[64]{0:T(128)} %param.15) | copy-start | bytes 772
  104.5 93.0 %copy-start.1 = (f32[2,1024]{1,0:T(2,128)S(1)}, f32[2,1024]{1,0:T(2,128)}, u32[]{:S(2)}) copy-start(f32[2,1024]{1,0:T(2,128)} %param.13) | copy-start | bytes 24580
  210.0 8.9 %all-to-all-start.1 = ((f32[8,4,512]{2,1,0:T(4,128)}), f32[8,4,512]{2,1,0:T(4,128)S(1)}, u32[]{:S(2)}, u32[]{:S(2)}) async-start(f32[8,4,512]{2,1,0:T(4,128)} %pad_maximum_fusion), calls=%async_computation.1 | async-start | bytes 131072 | tf_op jit(solution)/shard_map/all_to_all | solution.py:163
  213.4 203.1 %all-reduce.5.cloned.1.call-start = ((), (), s32[]{:S(2)}) async-start(), calls=%async_computation.2 | async-start | bytes 2097152
  233.1 36.6 %copy-start.5 = (u32[256]{0:T(256)S(1)}, u32[256]{0:T(256)}, u32[]{:S(2)}) copy-start(u32[256]{0:T(256)} %constant.165) | copy-start | bytes 3076
Sparse Core Ops, SparseCore 0:
  268.9 147.4 all-reduce.4
where the time goes:
time: 428 us; the launch traced here: 425 us
  waiting for transfers between devices  151 us (35%)
  other arithmetic  96.2 us (22%)
  blocking collectives  89.1 us (21%)
  matrix products  32.4 us (8%)
  local copies, waits for them, and re-layouts  31.9 us (7%)
  between operations  15 us (4%)
  starting transfers between devices  7.86 us (2%)
    unnamed x2, waiting for transfers between devices  146 us
    all_gather x8, blocking collectives, whole_of(): result = lax.all_gather(result, axes[number], axis=dim, tiled=True)  89.1 us
    dot_general x1, other arithmetic, predict_piece(): lax.dot_general(sine_table, spec_piece, contract_dims, preferred_element_...  35.5 us
    dot_general x1, other arithmetic, predict_piece(): lax.dot_general(cosine, spec_piece, contract_dims, preferred_element_type...  35.1 us
    dot_general x16, matrix products, block_term(): jnp.einsum('cbv,bu->vcu', left_table, block_data[0], preferred_element_ty...  25.3 us
    convert_element_type x1, other arithmetic, spread_rows(): return place_taps(offset, kernel_weights(col_frac)).astype(jnp.bfloat16)  13.5 us
    gather x2, local copies, waits for them, and re-layouts, on_device(): gathered = jnp.take(float_rows, slot_index, axis=1).transpose(1, 0, 2)  11.4 us
    gather x2, local copies, waits for them, and re-layouts, on_device(): packed_cells = jnp.take(cell_rows, slot_index, axis=1).transpose(1, 0, 2)  11.4 us
  transfers between devices with their start and end apart: 3, of which 2 were waited for; matrix products, arithmetic and copies ran while one was open for 22% of the time, Pallas kernels for 0%

commit v1 on v0

v1 whole, which is shorter than its diff:
```python
import jax
import jax.numpy as jnp
from jax import lax
from jax.experimental import pallas as pl
from jax.experimental.pallas import tpu as pltpu
from jax.sharding import Mesh
from jax.sharding import PartitionSpec as P

GRID = 8192
BAND = 128
TAPS = 8
TILE = ("tile_0", "tile_1")
VIS = ("vis_0", "vis_1")
VIS_TILE = ("vis_0", "vis_1", "tile_0", "tile_1")
DIGIT_LANE = 64
F32 = jnp.float32
BF16 = jnp.bfloat16
NT = (((1,), (1,)), ((), ()))
NN = (((1,), (0,)), ((), ()))

COS_POLY = (1.4142135, -6.97885099, 5.73946112, -1.88356261, 0.31069733)
SIN_POLY = (4.4428679, -7.30744333, 3.59478717, -0.78437159)
ROUND = 12582912.0


def three_parts(value):
    first = value.astype(BF16).astype(F32)
    rest = value - first
    second = rest.astype(BF16).astype(F32)
    return [first, second, rest - second]


def component_rows(spectra, positions):
    low = ((positions + 64) & 127) - 64
    high = (positions - low) >> 7
    digits = jnp.concatenate(
        [
            jnp.broadcast_to(d[None], (n, d.shape[0]))
            for d, n in ((high[0], 4), (low[0], 5), (high[1], 4), (low[1], 5))
        ]
    ).astype(BF16)
    rows = jnp.concatenate([spectra, digits])
    return jnp.pad(rows, ((0, 128 - rows.shape[0]), (0, 0))).T


def row_factors(cells, fractions):
    parts = []
    for axis in range(2):
        first = cells[axis : axis + 1] + 3
        low = ((first + 32) & 63) - 32
        high = first - low
        frac = three_parts(fractions[axis : axis + 1])
        parts += [low.astype(F32) * (128.0 / GRID)] + [f * (128.0 / GRID) for f in frac]
        high = ((high + GRID // 2) & (GRID - 1)) - GRID // 2
        parts += [high.astype(F32) * (1.0 / GRID), low.astype(F32) * (1.0 / GRID)]
        parts += [f * (1.0 / GRID) for f in frac]
    return parts


def polynomial(coefficients, s):
    result = coefficients[-1] * s + coefficients[-2]
    for c in coefficients[-3::-1]:
        result = result * s + c
    return result


def predict_kernel(counts, comps, cells, fractions, observed, weights, residual, packed, factors, fields):
    rows = observed.shape[0]
    slot = packed.shape[2]
    tiles = packed.shape[0]
    comp_total = comps.shape[0]
    parts = row_factors(cells[...], fractions[...])
    lead = jnp.zeros((DIGIT_LANE, rows), F32)
    tail = jnp.zeros((128 - DIGIT_LANE - len(parts), rows), F32)
    factors[...] = jnp.concatenate([lead] + parts + [tail]).T.astype(BF16)

    start = []
    total = counts[0, 0] * 0
    for t in range(tiles):
        start.append(total)
        total = total + counts[0, t]

    w = weights[...]
    both = jnp.concatenate([w, w], axis=1)
    lane = lax.broadcasted_iota(jnp.int32, both.shape, 1)
    w_re = three_parts(jnp.where(lane < 64, both, 0.0))
    w_im = three_parts(jnp.where(lane < 64, 0.0, both))
    w_rows = jnp.concatenate(w_re + w_im + [jnp.zeros((2, 128), F32)]).astype(BF16)

    block = 256
    comp_block = 256

    def row_step(step, carry):
        at = pl.ds(step * block, block)
        left = factors[at, :]
        acc_cos = jnp.zeros((block, 128), F32)
        acc_sin = jnp.zeros((block, 128), F32)
        for k in range(comp_total // comp_block):
            piece = comps[k * comp_block : (k + 1) * comp_block, :]
            turns = lax.dot_general(left, piece, NT, preferred_element_type=F32)
            y = turns - ((turns + ROUND) - ROUND)
            s = y * y
            c = polynomial(COS_POLY, s)
            d = polynomial(SIN_POLY, s) * y
            cosine = (1.0 - d * d).astype(BF16)
            sine = (c * d).astype(BF16)
            acc_cos += lax.dot_general(cosine, piece, NN, preferred_element_type=F32)
            acc_sin += lax.dot_general(sine, piece, NN, preferred_element_type=F32)
        lanes = lax.broadcasted_iota(jnp.int32, (block, 128), 1)
        index = lax.broadcasted_iota(jnp.int32, (block, 128), 0) + step * block
        predicted = jnp.where(lanes < 64, acc_cos, -pltpu.roll(acc_sin, 64, 1))
        res = jnp.where(index < total, observed[at, :].astype(F32) - predicted, 0.0).astype(BF16)
        residual[at, :] = res
        sums = lax.dot_general(w_rows, res, NT, preferred_element_type=F32)
        fields[0:1, at] = sums[0:1] + sums[1:2] + sums[2:3]
        fields[1:2, at] = sums[3:4] + sums[4:5] + sums[5:6]
        return carry

    lax.fori_loop(0, rows // block, row_step, 0)
    fields[2:4, :] = fractions[...]
    fields[4:6, :] = cells[...].astype(F32)
    fields[6:8, :] = jnp.zeros((2, rows), F32)
    everything = fields[...]
    row_of = lax.broadcasted_iota(jnp.int32, (8, slot), 0)
    place = lax.broadcasted_iota(jnp.int32, (8, slot), 1)
    for t in range(tiles):
        moved = pltpu.roll(everything, (rows - start[t]) & (rows - 1), 1)[:, :slot]
        moved = jnp.where((row_of >= 2) | (place < counts[0, t]), moved, 0.0)
        base = float(t * (GRID // tiles))
        packed[t] = moved - jnp.where(row_of == 4, base, 0.0)


def grid_kernel(got, out, acc):
    sources, _, slot = got.shape
    width = acc.shape[1]
    high = acc.shape[0]
    scale = -0.7213475204444817
    acc[...] = jnp.zeros(acc.shape, F32)
    line = lax.broadcasted_iota(jnp.int32, (high, slot), 0)
    line_row = line >> 1
    imag = (line & 1) == 1

    def source_step(step, carry):
        data = got[step]
        first_row = data[5:6, :].astype(jnp.int32)
        value = jnp.where(imag, data[1:2, :], data[0:1, :])
        tap = line_row - first_row
        off = (tap - 3).astype(F32) - data[3:4, :]
        kernel = jnp.exp2(off * off * scale)
        left = jnp.where((tap & ~7) == 0, value * kernel, 0.0).astype(BF16)
        turned = data.T
        block = 128
        cols = []
        for r in range(slot // block):
            sub = turned[r * block : (r + 1) * block]
            first_col = sub[:, 4:5].astype(jnp.int32)
            col_frac = sub[:, 2:3]
            column = lax.broadcasted_iota(jnp.int32, (block, width), 1)
            tap_u = column - first_col
            off_u = (tap_u - 3).astype(F32) - col_frac
            weight = jnp.exp2(off_u * off_u * scale)
            cols.append(jnp.where((tap_u & ~7) == 0, weight, 0.0).astype(BF16))
        spread = jnp.concatenate(cols)
        acc[...] += lax.dot_general(left, spread, NN, preferred_element_type=F32)
        return carry

    lax.fori_loop(0, sources, source_step, 0)
    out[...] = acc[...].astype(BF16).reshape(out.shape)


def on_device(spectra, positions, observed, cells, fractions, bucket_counts, chan_weights):
    rows = observed.shape[0]
    tiles = lax.axis_size(TILE)
    owners = lax.axis_size(VIS)
    slot = rows // 2
    width = GRID // tiles
    devices = tiles * owners
    mine = component_rows(spectra, positions)
    comps = lax.all_to_all(
        jnp.broadcast_to(mine[None], (devices,) + mine.shape), VIS_TILE, 0, 0, tiled=True
    ).reshape(devices * mine.shape[0], 128)
    vmem = pl.BlockSpec(memory_space=pltpu.VMEM)
    residual, packed = pl.pallas_call(
        predict_kernel,
        out_shape=(
            jax.ShapeDtypeStruct(observed.shape, BF16),
            jax.ShapeDtypeStruct((tiles, 8, slot), F32),
        ),
        in_specs=[pl.BlockSpec(memory_space=pltpu.SMEM)] + [vmem] * 5,
        out_specs=(vmem, vmem),
        scratch_shapes=[pltpu.VMEM((rows, 128), BF16), pltpu.VMEM((8, rows), F32)],
        name="predict",
    )(bucket_counts, comps, cells, fractions, observed, chan_weights[None, :])
    got = lax.all_to_all(packed, TILE, 0, 0, tiled=True)
    share = BAND // owners
    partial = pl.pallas_call(
        grid_kernel,
        out_shape=jax.ShapeDtypeStruct((owners, 2 * share, width), BF16),
        in_specs=[vmem],
        out_specs=vmem,
        scratch_shapes=[pltpu.VMEM((2 * BAND, width), F32)],
        name="gridding",
    )(got)
    parts = lax.all_to_all(partial, VIS, 0, 0, tiled=True)
    total = jnp.sum(parts.astype(F32), axis=0)
    return residual, total.reshape(share, 2, width)


def solution(mesh):
    torus = Mesh(mesh.devices.reshape(4, 8, 4, 2), ("vis_0", "vis_1", "tile_0", "tile_1"))
    return jax.shard_map(
        on_device,
        mesh=torus,
        in_specs=(
            P(None, VIS_TILE),
            P(None, VIS_TILE),
            P(VIS_TILE, None),
            P(None, VIS_TILE),
            P(None, VIS_TILE),
            P(VIS_TILE, None),
            P(),
        ),
        out_specs=(P(VIS_TILE, None), P(VIS, None, TILE)),
        check_vma=False,
    )
```

time: 428 us -> 97 us (0.23)
  waiting for transfers between devices: 151 us -> 0 us
  other arithmetic: 96.2 us -> 0.78 us
  matrix products: 32.4 us -> 0 us
  local copies, waits for them, and re-layouts: 31.9 us -> 1.71 us
  Pallas kernels: 0 us -> 26.5 us
  blocking collectives: 89.1 us -> 66.9 us
  between operations: 15 us -> 0.64 us
  starting transfers between devices: 7.86 us -> 0 us
    unnamed x2 -> x0, waiting for transfers between devices: 146 us -> none
    all_gather x8 -> x0, blocking collectives: 89.1 us -> none  [whole_of(): result = lax.all_gather(result, axes[number], axis=dim, tiled=True)]
    dot_general x2 -> x0, other arithmetic: 70.5 us -> none  [the longest x1 35.5 us: predict_piece(): lax.dot_general(sine_table, spec_piece, contract_dims, preferred_element_...]
    all_to_all x0 -> x3, blocking collectives: none -> 66.9 us  [the longest x1 33.9 us: on_device(): lax.all_to_all(jnp.broadcast_to(mine[None], (devices,) + mine.shape), VIS...]
    dot_general x18 -> x0, matrix products: 32.4 us -> none  [the longest x16 25.3 us: block_term(): jnp.einsum('cbv,bu->vcu', left_table, block_data[0], preferred_element_ty...]
    pallas_call x0 -> x2, Pallas kernels: none -> 26.5 us  [the longest x1 13.4 us: on_device(): pl.pallas_call(predict_kernel, out_shape=(jax.ShapeDtypeStruct(observed.s...]
    gather x4 -> x0, local copies, waits for them, and re-layouts: 22.8 us -> none  [the longest x2 11.4 us: on_device(): gathered = jnp.take(float_rows, slot_index, axis=1).transpose(1, 0, 2)]
    convert_element_type x2 -> x0, other arithmetic: 13.6 us -> none  [the longest x1 13.5 us: spread_rows(): return place_taps(offset, kernel_weights(col_frac)).astype(jnp.bfloat16)]
  transfers between devices with their start and end apart: 3 -> 0, of which waited for: 2 -> 0; matrix products, arithmetic and copies ran while one was open for 22% -> 0% of each run, Pallas kernels for 0% -> 0%
where the time goes in v1:
time: 97 us; the launch traced here: 96.6 us
  blocking collectives  66.9 us (69%)
  Pallas kernels  26.5 us (27%)
  local copies, waits for them, and re-layouts  1.71 us (2%)
    all_to_all x1, blocking collectives, on_device(): lax.all_to_all(jnp.broadcast_to(mine[None], (devices,) + mine.shape), VIS...  33.9 us
    all_to_all x1, blocking collectives, on_device(): parts = lax.all_to_all(partial, VIS, 0, 0, tiled=True)  22.9 us
    pallas_call x1, Pallas kernels, on_device(): pl.pallas_call(predict_kernel, out_shape=(jax.ShapeDtypeStruct(observed.s...  13.4 us
    pallas_call x1, Pallas kernels, on_device(): pl.pallas_call(grid_kernel, out_shape=jax.ShapeDtypeStruct((owners, 2 * s...  13.1 us
    all_to_all x1, blocking collectives, on_device(): got = lax.all_to_all(packed, TILE, 0, 0, tiled=True)  10.1 us

profile of v1, /device:TPU:32, one launch (start us, length us, event | category | flops | bytes accessed | tf_op | source)
XLA Modules:
  0.0 96.6 jit_solution(526212241985548625)
XLA Ops:
  0.6 0.7 and_add_fusion
  1.3 0.1 broadcast_in_dim.44
  1.4 0.1 broadcast_in_dim.40
  1.5 0.1 broadcast_in_dim.38
  1.5 0.0 copy-start
  1.5 0.1 broadcast_in_dim.42
  1.6 0.6 copy-done
  2.2 0.1 concatenate.6
  2.3 0.1 broadcast_in_dim.45
  2.4 33.9 %all_to_all.15 = bf16[256,8,128]{2,1,0:T(8,128)(2,1)} all-to-all(bf16[256,8,128]{2,1,0:T(8,128)(2,1)S(1)} %broadcast_in_dim.45), channel_id=1, replica_groups=mesh['vis_0'=4,'vis_1'=8,'tile_0'=4,'tile_1'=2] {'vis_0','vis_1','tile_0..., dimensions={0} | all-to-all | bytes 1048576 | tf_op jit(solution)/shard_map/all_to_all | solution.py:179
  36.3 13.4 %predict.1 = (bf16[1024,128]{1,0:T(8,128)(2,1)}, f32[8,8,512]{2,1,0:T(8,128)}) custom-call(s32[1,8]{1,0:T(1,128)} %counts.1, bf16[2048,128]{1,0:T(8,128)(2,1)} %bitcast.12, s32[2,1024]{1,0:T(2,128)} %cells.1, f32[2,1024]{1,0:T(2,128)} %fractions.1, bf16[1024,128]{1,0:T(8,128)(2,1)} %observed.1, f32[1,64]{1,0:T(1,128)} %bitcast.13), custom_call_target="tpu_custom_call" | custom-call | tf_op jit(solution)/shard_map/predict/pallas_call | solution.py:183
  49.7 10.1 %all_to_all.16.got = f32[8,8,512]{2,1,0:T(8,128)} all-to-all(f32[8,8,512]{2,1,0:T(8,128)} %get-tuple-element.5), channel_id=1, replica_groups=mesh['vis_0'=4,'vis_1'=8,'tile_0'=4,'tile_1'=2] {'tile_0','tile_1'}, dimensions={0} | all-to-all | bytes 262144 | tf_op jit(solution)/shard_map/all_to_all | solution.py:194
  59.8 13.1 %gridding.1 = bf16[32,8,1024]{2,1,0:T(8,128)(2,1)} custom-call(f32[8,8,512]{2,1,0:T(8,128)} %all_to_all.16.got), custom_call_target="tpu_custom_call" | custom-call | tf_op jit(solution)/shard_map/gridding/pallas_call | solution.py:196
  72.9 22.9 %all_to_all.17 = bf16[32,8,1024]{2,1,0:T(8,128)(2,1)S(1)} all-to-all(bf16[32,8,1024]{2,1,0:T(8,128)(2,1)} %gridding.1), channel_id=1, replica_groups=mesh['vis_0'=4,'vis_1'=8,'tile_0'=4,'tile_1'=2] {'vis_0','vis_1'}, dimensions={0} | all-to-all | bytes 1048576 | tf_op jit(solution)/shard_map/all_to_all | solution.py:204
  95.8 0.1 convert_reduce_fusion
  95.9 0.6 reshape.12
  (2 shorter events, 0.0 us)
Async XLA Ops:
  1.5 0.7 copy-start

commit v2 on v1

--- a/solution.py
+++ b/solution.py
@@ -18,7 +18,7 @@
 NT = (((1,), (1,)), ((), ()))
 NN = (((1,), (0,)), ((), ()))
 
-COS_POLY = (1.4142135, -6.97885099, 5.73946112, -1.88356261, 0.31069733)
+COS_POLY = (1.41420408, -6.97764191, 5.71523647, -1.72834251)
 SIN_POLY = (4.4428679, -7.30744333, 3.59478717, -0.78437159)
 ROUND = 12582912.0
 
@@ -57,6 +57,14 @@
     return parts
 
 
+def monic(coefficients, s):
+    lead = coefficients[-1]
+    result = s + coefficients[-2] / lead
+    for c in coefficients[-3::-1]:
+        result = result * s + c / lead
+    return result
+
+
 def polynomial(coefficients, s):
     result = coefficients[-1] * s + coefficients[-2]
     for c in coefficients[-3::-1]:
@@ -64,11 +72,11 @@
     return result
 
 
-def predict_kernel(counts, comps, cells, fractions, observed, weights, residual, packed, factors, fields):
+def predict_kernel(counts, here, there, cells, fractions, observed, weights, residual, packed, factors, fields):
     rows = observed.shape[0]
     slot = packed.shape[2]
     tiles = packed.shape[0]
-    comp_total = comps.shape[0]
+    comp_total = here.shape[0]
     parts = row_factors(cells[...], fractions[...])
     lead = jnp.zeros((DIGIT_LANE, rows), F32)
     tail = jnp.zeros((128 - DIGIT_LANE - len(parts), rows), F32)
@@ -87,7 +95,7 @@
     w_im = three_parts(jnp.where(lane < 64, 0.0, both))
     w_rows = jnp.concatenate(w_re + w_im + [jnp.zeros((2, 128), F32)]).astype(BF16)
 
-    block = 256
+    block = 1024
     comp_block = 256
 
     def row_step(step, carry):
@@ -95,20 +103,22 @@
         left = factors[at, :]
         acc_cos = jnp.zeros((block, 128), F32)
         acc_sin = jnp.zeros((block, 128), F32)
-        for k in range(comp_total // comp_block):
-            piece = comps[k * comp_block : (k + 1) * comp_block, :]
+        for k in range(2 * comp_total // comp_block):
+            comps = here if k * comp_block < comp_total else there
+            piece_at = k * comp_block % comp_total
+            piece = comps[piece_at : piece_at + comp_block, :]
             turns = lax.dot_general(left, piece, NT, preferred_element_type=F32)
             y = turns - ((turns + ROUND) - ROUND)
             s = y * y
-            c = polynomial(COS_POLY, s)
-            d = polynomial(SIN_POLY, s) * y
-            cosine = (1.0 - d * d).astype(BF16)
+            c = monic(COS_POLY, s)
+            d = monic(SIN_POLY, s) * y
+            cosine = (1.0 / SIN_POLY[-1] ** 2 - d * d).astype(BF16)
             sine = (c * d).astype(BF16)
             acc_cos += lax.dot_general(cosine, piece, NN, preferred_element_type=F32)
             acc_sin += lax.dot_general(sine, piece, NN, preferred_element_type=F32)
         lanes = lax.broadcasted_iota(jnp.int32, (block, 128), 1)
         index = lax.broadcasted_iota(jnp.int32, (block, 128), 0) + step * block
-        predicted = jnp.where(lanes < 64, acc_cos, -pltpu.roll(acc_sin, 64, 1))
+        predicted = jnp.where(lanes < 64, acc_cos * SIN_POLY[-1] ** 2, pltpu.roll(acc_sin, 64, 1) * (-COS_POLY[-1] * SIN_POLY[-1]))
         res = jnp.where(index < total, observed[at, :].astype(F32) - predicted, 0.0).astype(BF16)
         residual[at, :] = res
         sums = lax.dot_general(w_rows, res, NT, preferred_element_type=F32)
@@ -132,34 +142,35 @@
 
 def grid_kernel(got, out, acc):
     sources, _, slot = got.shape
+    slot = slot * 4
+    sources = sources // 4
     width = acc.shape[1]
     high = acc.shape[0]
     scale = -0.7213475204444817
     acc[...] = jnp.zeros(acc.shape, F32)
     line = lax.broadcasted_iota(jnp.int32, (high, slot), 0)
     line_row = line >> 1
+    line_float = line_row.astype(F32)
     imag = (line & 1) == 1
+    block = 128
+    column = lax.broadcasted_iota(jnp.int32, (block, width), 1)
+    column_float = column.astype(F32)
 
     def source_step(step, carry):
-        data = got[step]
-        first_row = data[5:6, :].astype(jnp.int32)
+        data = jnp.concatenate([got[step * 4 + k] for k in range(4)], axis=1)
         value = jnp.where(imag, data[1:2, :], data[0:1, :])
-        tap = line_row - first_row
-        off = (tap - 3).astype(F32) - data[3:4, :]
+        off = line_float - (data[5:6, :] + 3.0 + data[3:4, :])
         kernel = jnp.exp2(off * off * scale)
-        left = jnp.where((tap & ~7) == 0, value * kernel, 0.0).astype(BF16)
-        turned = data.T
-        block = 128
+        near = (lambda t: t.astype(jnp.uint32) < 8)(line_row - data[5:6, :].astype(jnp.int32))
+        left = jnp.where(near, value * kernel, 0.0).astype(BF16)
+        turned = jnp.concatenate([data[4:5], data[4:5] + 3.0 + data[2:3], data[:6]]).T
         cols = []
         for r in range(slot // block):
             sub = turned[r * block : (r + 1) * block]
-            first_col = sub[:, 4:5].astype(jnp.int32)
-            col_frac = sub[:, 2:3]
-            column = lax.broadcasted_iota(jnp.int32, (block, width), 1)
-            tap_u = column - first_col
-            off_u = (tap_u - 3).astype(F32) - col_frac
+            first_col = sub[:, 0:1].astype(jnp.int32)
+            off_u = column_float - sub[:, 1:2]
             weight = jnp.exp2(off_u * off_u * scale)
-            cols.append(jnp.where((tap_u & ~7) == 0, weight, 0.0).astype(BF16))
+            cols.append(jnp.where((lambda t: t.astype(jnp.uint32) < 8)(column - first_col), weight, 0.0).astype(BF16))
         spread = jnp.concatenate(cols)
         acc[...] += lax.dot_general(left, spread, NN, preferred_element_type=F32)
         return carry
@@ -176,9 +187,12 @@
     width = GRID // tiles
     devices = tiles * owners
     mine = component_rows(spectra, positions)
-    comps = lax.all_to_all(
-        jnp.broadcast_to(mine[None], (devices,) + mine.shape), VIS_TILE, 0, 0, tiled=True
-    ).reshape(devices * mine.shape[0], 128)
+    same_core = VIS + ("tile_0",)
+    half = devices // lax.axis_size("tile_1")
+    here = lax.all_to_all(
+        jnp.broadcast_to(mine[None], (half,) + mine.shape), same_core, 0, 0, tiled=True
+    ).reshape(half * mine.shape[0], 128)
+    there = lax.ppermute(here, "tile_1", [(0, 1), (1, 0)])
     vmem = pl.BlockSpec(memory_space=pltpu.VMEM)
     residual, packed = pl.pallas_call(
         predict_kernel,
@@ -186,11 +200,11 @@
             jax.ShapeDtypeStruct(observed.shape, BF16),
             jax.ShapeDtypeStruct((tiles, 8, slot), F32),
         ),
-        in_specs=[pl.BlockSpec(memory_space=pltpu.SMEM)] + [vmem] * 5,
+        in_specs=[pl.BlockSpec(memory_space=pltpu.SMEM)] + [vmem] * 6,
         out_specs=(vmem, vmem),
         scratch_shapes=[pltpu.VMEM((rows, 128), BF16), pltpu.VMEM((8, rows), F32)],
         name="predict",
-    )(bucket_counts, comps, cells, fractions, observed, chan_weights[None, :])
+    )(bucket_counts, here, there, cells, fractions, observed, chan_weights[None, :])
     got = lax.all_to_all(packed, TILE, 0, 0, tiled=True)
     share = BAND // owners
     partial = pl.pallas_call(

time: 97 us -> 84.7 us (0.87)
  Pallas kernels: 26.5 us -> 17.3 us
  blocking collectives: 66.9 us -> 61.7 us
  waiting for transfers between devices: 0 us -> 1.53 us
    pallas_call x1, Pallas kernels: 13.4 us -> 8.43 us  [on_device(): pl.pallas_call(predict_kernel, out_shape=(jax.ShapeDtypeStruct(observed.s...]
    all_to_all x1, blocking collectives: 33.9 us -> 29 us  [on_device(): lax.all_to_all(jnp.broadcast_to(mine[None], (half,) + mine.shape), same_c...]
    pallas_call x1, Pallas kernels: 13.1 us -> 8.86 us  [on_device(): pl.pallas_call(grid_kernel, out_shape=jax.ShapeDtypeStruct((owners, 2 * s...]
    ppermute x0 -> x1, waiting for transfers between devices: none -> 1.53 us  [on_device(): there = lax.ppermute(here, 'tile_1', [(0, 1), (1, 0)])]
  transfers between devices with their start and end apart: 0 -> 1, of which waited for: 0 -> 1; matrix products, arithmetic and copies ran while one was open for 0% -> 0% of each run, Pallas kernels for 0% -> 0%
where the time goes in v2:
time: 84.7 us; the launch traced here: 84.3 us
  blocking collectives  61.7 us (73%)
  Pallas kernels  17.3 us (20%)
  local copies, waits for them, and re-layouts  2.38 us (3%)
  waiting for transfers between devices  1.53 us (2%)
    all_to_all x1, blocking collectives, on_device(): lax.all_to_all(jnp.broadcast_to(mine[None], (half,) + mine.shape), same_c...  29 us
    all_to_all x1, blocking collectives, on_device(): parts = lax.all_to_all(partial, VIS, 0, 0, tiled=True)  22.6 us
    all_to_all x1, blocking collectives, on_device(): got = lax.all_to_all(packed, TILE, 0, 0, tiled=True)  10.1 us
    pallas_call x1, Pallas kernels, on_device(): pl.pallas_call(grid_kernel, out_shape=jax.ShapeDtypeStruct((owners, 2 * s...  8.86 us
    pallas_call x1, Pallas kernels, on_device(): pl.pallas_call(predict_kernel, out_shape=(jax.ShapeDtypeStruct(observed.s...  8.43 us
  transfers between devices with their start and end apart: 1, of which 1 were waited for; matrix products, arithmetic and copies ran while one was open for 0% of the time, Pallas kernels for 0%

profile of v2, /device:TPU:32, one launch (start us, length us, event | category | flops | bytes accessed | tf_op | source)
XLA Modules:
  0.0 84.3 jit_solution(1847439098189732368)
XLA Ops:
  0.6 0.7 and_add_fusion
  1.3 0.1 broadcast_in_dim.44
  1.4 0.1 broadcast_in_dim.40
  1.5 0.1 broadcast_in_dim.38
  1.5 0.0 copy-start.2
  1.5 0.1 broadcast_in_dim.42
  1.6 0.6 copy-done.2
  2.2 0.1 concatenate.6
  2.4 29.0 %all_to_all.15 = bf16[128,8,128]{2,1,0:T(8,128)(2,1)S(1)} all-to-all(bf16[128,8,128]{2,1,0:T(8,128)(2,1)S(1)} %broadcast_in_dim.45), channel_id=1, replica_groups=mesh['vis_0'=4,'vis_1'=8,'tile_0'=4,'tile_1'=2] {'vis_0','vis_1','tile_0'}, dimensions={0} | all-to-all | bytes 524288 | tf_op jit(solution)/shard_map/all_to_all | solution.py:192
  31.4 0.0 copy-start
  31.4 0.0 collective-permute-start
  31.4 1.5 %collective-permute-done.there = bf16[1024,128]{1,0:T(8,128)(2,1)S(1)} collective-permute-done((bf16[1024,128]{1,0:T(8,128)(2,1)S(1)}, bf16[1024,128]{1,0:T(8,128)(2,1)S(1)}, u32[]{:S(2)}, u32[]{:S(2)}) %collective-permute-start) | collective-permute-done | bytes 262176 | tf_op jit(solution)/shard_map/ppermute | solution.py:195
  32.9 0.0 copy-start.1
  32.9 0.0 copy-done
  32.9 0.7 copy-done.1
  33.6 8.4 %predict.1 = (bf16[1024,128]{1,0:T(8,128)(2,1)}, f32[8,8,512]{2,1,0:T(8,128)}) custom-call(s32[1,8]{1,0:T(1,128)} %counts.1, bf16[1024,128]{1,0:T(8,128)(2,1)} %bitcast.13, bf16[1024,128]{1,0:T(8,128)(2,1)} %copy-done.1, s32[2,1024]{1,0:T(2,128)} %cells.1, f32[2,1024]{1,0:T(2,128)} %fractions.1, bf16[1024,128]{1,0:T(8,128)(2,1)} %observed.1, f32[1,64]{1,0:T(1,128)} %bitcast.14), custom_call_target="tpu_custom_call" | custom-call | tf_op jit(solution)/shard_map/predict/pallas_call | solution.py:197
  42.1 10.1 %all_to_all.16.got = f32[8,8,512]{2,1,0:T(8,128)} all-to-all(f32[8,8,512]{2,1,0:T(8,128)} %get-tuple-element.5), channel_id=1, replica_groups=mesh['vis_0'=4,'vis_1'=8,'tile_0'=4,'tile_1'=2] {'tile_0','tile_1'}, dimensions={0} | all-to-all | bytes 262144 | tf_op jit(solution)/shard_map/all_to_all | solution.py:208
  52.1 8.9 %gridding.1 = bf16[32,8,1024]{2,1,0:T(8,128)(2,1)} custom-call(f32[8,8,512]{2,1,0:T(8,128)} %all_to_all.16.got), custom_call_target="tpu_custom_call" | custom-call | tf_op jit(solution)/shard_map/gridding/pallas_call | solution.py:210
  61.0 22.6 %all_to_all.17 = bf16[32,8,1024]{2,1,0:T(8,128)(2,1)S(1)} all-to-all(bf16[32,8,1024]{2,1,0:T(8,128)(2,1)} %gridding.1), channel_id=1, replica_groups=mesh['vis_0'=4,'vis_1'=8,'tile_0'=4,'tile_1'=2] {'vis_0','vis_1'}, dimensions={0} | all-to-all | bytes 1048576 | tf_op jit(solution)/shard_map/all_to_all | solution.py:218
  83.6 0.1 convert_reduce_fusion
  83.7 0.6 reshape.12
  (3 shorter events, 0.1 us)
Async XLA Ops:
  1.5 0.7 copy-start.2
  31.4 1.5 %copy-start = (bf16[128,8,128]{2,1,0:T(8,128)(2,1)}, bf16[128,8,128]{2,1,0:T(8,128)(2,1)S(1)}, u32[]{:S(2)}) copy-start(bf16[128,8,128]{2,1,0:T(8,128)(2,1)S(1)} %all_to_all.15) | copy-start | bytes 786436
  31.4 1.5 %collective-permute-start = (bf16[1024,128]{1,0:T(8,128)(2,1)S(1)}, bf16[1024,128]{1,0:T(8,128)(2,1)S(1)}, u32[]{:S(2)}, u32[]{:S(2)}) collective-permute-start(bf16[1024,128]{1,0:T(8,128)(2,1)S(1)} %bitcast.12), channel_id=1, source_target_pairs={{0,1},{1,0},{2,3},{3,2},{4,5},{5,4},{6,7},{7,6},{8,9},{9,8},{10,11... | collective-permute-start | bytes 786440 | tf_op jit(solution)/shard_map/ppermute | solution.py:195
  32.9 0.7 copy-start.1

commit v3 on v2

--- a/solution.py
+++ b/solution.py
@@ -20,6 +20,7 @@
 
 COS_POLY = (1.41420408, -6.97764191, 5.71523647, -1.72834251)
 SIN_POLY = (4.4428679, -7.30744333, 3.59478717, -0.78437159)
+LIMIT = pltpu.CompilerParams(vmem_limit_bytes=24 * 2**20)
 ROUND = 12582912.0
 
 
@@ -72,16 +73,44 @@
     return result
 
 
-def predict_kernel(counts, here, there, cells, fractions, observed, weights, residual, packed, factors, fields):
+def add_products(left, comps, cos_sum, sin_sum):
+    comp_block = 256
+    for first in range(0, comps.shape[0], comp_block):
+        piece = comps[first : first + comp_block, :]
+        turns = lax.dot_general(left, piece, NT, preferred_element_type=F32)
+        y = turns - ((turns + ROUND) - ROUND)
+        s = y * y
+        c = monic(COS_POLY, s)
+        d = monic(SIN_POLY, s) * y
+        cosine = (1.0 / SIN_POLY[-1] ** 2 - d * d).astype(BF16)
+        sine = (c * d).astype(BF16)
+        cos_sum += lax.dot_general(cosine, piece, NN, preferred_element_type=F32)
+        sin_sum += lax.dot_general(sine, piece, NN, preferred_element_type=F32)
+    return cos_sum, sin_sum
+
+
+def first_kernel(*refs):
+    pieces, (cells, fractions, factors, cos_out, sin_out) = refs[:-5], refs[-5:]
+    rows = factors.shape[0]
+    parts = row_factors(cells[...], fractions[...])
+    lead = jnp.zeros((DIGIT_LANE, rows), F32)
+    tail = jnp.zeros((128 - DIGIT_LANE - len(parts), rows), F32)
+    left = jnp.concatenate([lead] + parts + [tail]).T.astype(BF16)
+    factors[...] = left
+    cos_sum = jnp.zeros((rows, 128), F32)
+    sin_sum = jnp.zeros((rows, 128), F32)
+    for comps in pieces:
+        cos_sum, sin_sum = add_products(left, comps, cos_sum, sin_sum)
+    cos_out[...] = cos_sum
+    sin_out[...] = sin_sum
+
+
+def second_kernel(
+    counts, comps, factors, cos_in, sin_in, cells, fractions, observed, weights, residual, packed, fields
+):
     rows = observed.shape[0]
     slot = packed.shape[2]
     tiles = packed.shape[0]
-    comp_total = here.shape[0]
-    parts = row_factors(cells[...], fractions[...])
-    lead = jnp.zeros((DIGIT_LANE, rows), F32)
-    tail = jnp.zeros((128 - DIGIT_LANE - len(parts), rows), F32)
-    factors[...] = jnp.concatenate([lead] + parts + [tail]).T.astype(BF16)
-
     start = []
     total = counts[0, 0] * 0
     for t in range(tiles):
@@ -95,38 +124,17 @@
     w_im = three_parts(jnp.where(lane < 64, 0.0, both))
     w_rows = jnp.concatenate(w_re + w_im + [jnp.zeros((2, 128), F32)]).astype(BF16)
 
-    block = 1024
-    comp_block = 256
-
-    def row_step(step, carry):
-        at = pl.ds(step * block, block)
-        left = factors[at, :]
-        acc_cos = jnp.zeros((block, 128), F32)
-        acc_sin = jnp.zeros((block, 128), F32)
-        for k in range(2 * comp_total // comp_block):
-            comps = here if k * comp_block < comp_total else there
-            piece_at = k * comp_block % comp_total
-            piece = comps[piece_at : piece_at + comp_block, :]
-            turns = lax.dot_general(left, piece, NT, preferred_element_type=F32)
-            y = turns - ((turns + ROUND) - ROUND)
-            s = y * y
-            c = monic(COS_POLY, s)
-            d = monic(SIN_POLY, s) * y
-            cosine = (1.0 / SIN_POLY[-1] ** 2 - d * d).astype(BF16)
-            sine = (c * d).astype(BF16)
-            acc_cos += lax.dot_general(cosine, piece, NN, preferred_element_type=F32)
-            acc_sin += lax.dot_general(sine, piece, NN, preferred_element_type=F32)
-        lanes = lax.broadcasted_iota(jnp.int32, (block, 128), 1)
-        index = lax.broadcasted_iota(jnp.int32, (block, 128), 0) + step * block
-        predicted = jnp.where(lanes < 64, acc_cos * SIN_POLY[-1] ** 2, pltpu.roll(acc_sin, 64, 1) * (-COS_POLY[-1] * SIN_POLY[-1]))
-        res = jnp.where(index < total, observed[at, :].astype(F32) - predicted, 0.0).astype(BF16)
-        residual[at, :] = res
-        sums = lax.dot_general(w_rows, res, NT, preferred_element_type=F32)
-        fields[0:1, at] = sums[0:1] + sums[1:2] + sums[2:3]
-        fields[1:2, at] = sums[3:4] + sums[4:5] + sums[5:6]
-        return carry
-
-    lax.fori_loop(0, rows // block, row_step, 0)
+    cos_sum, sin_sum = add_products(factors[...], comps, cos_in[...], sin_in[...])
+    lanes = lax.broadcasted_iota(jnp.int32, (rows, 128), 1)
+    index = lax.broadcasted_iota(jnp.int32, (rows, 128), 0)
+    real = cos_sum * SIN_POLY[-1] ** 2
+    imag = pltpu.roll(sin_sum, 64, 1) * (-COS_POLY[-1] * SIN_POLY[-1])
+    predicted = jnp.where(lanes < 64, real, imag)
+    res = jnp.where(index < total, observed[...].astype(F32) - predicted, 0.0).astype(BF16)
+    residual[...] = res
+    sums = lax.dot_general(w_rows, res, NT, preferred_element_type=F32)
+    fields[0:1, :] = sums[0:1] + sums[1:2] + sums[2:3]
+    fields[1:2, :] = sums[3:4] + sums[4:5] + sums[5:6]
     fields[2:4, :] = fractions[...]
     fields[4:6, :] = cells[...].astype(F32)
     fields[6:8, :] = jnp.zeros((2, rows), F32)
@@ -187,24 +195,42 @@
     width = GRID // tiles
     devices = tiles * owners
     mine = component_rows(spectra, positions)
-    same_core = VIS + ("tile_0",)
-    half = devices // lax.axis_size("tile_1")
-    here = lax.all_to_all(
-        jnp.broadcast_to(mine[None], (half,) + mine.shape), same_core, 0, 0, tiled=True
-    ).reshape(half * mine.shape[0], 128)
-    there = lax.ppermute(here, "tile_1", [(0, 1), (1, 0)])
+    plane = ("vis_1", "tile_0")
+    members = lax.axis_size(plane)
+    own = lax.all_to_all(
+        jnp.broadcast_to(mine[None], (members,) + mine.shape), plane, 0, 0, tiled=True
+    ).reshape(members * mine.shape[0], 128)
+    line = lax.axis_size("vis_0")
+    here = [own] + [
+        lax.ppermute(own, "vis_0", [(k, (k + step) % line) for k in range(line)])
+        for step in range(1, line)
+    ]
+    there = lax.ppermute(jnp.concatenate(here), "tile_1", [(0, 1), (1, 0)])
     vmem = pl.BlockSpec(memory_space=pltpu.VMEM)
+    sums = jax.ShapeDtypeStruct((rows, 128), F32)
+    factors, cos_sum, sin_sum = pl.pallas_call(
+        first_kernel,
+        out_shape=(jax.ShapeDtypeStruct((rows, 128), BF16), sums, sums),
+        in_specs=[vmem] * (line + 2),
+        out_specs=(vmem,) * 3,
+        name="predict_first",
+        compiler_params=LIMIT,
+    )(*here, cells, fractions)
     residual, packed = pl.pallas_call(
-        predict_kernel,
+        second_kernel,
         out_shape=(
             jax.ShapeDtypeStruct(observed.shape, BF16),
             jax.ShapeDtypeStruct((tiles, 8, slot), F32),
         ),
-        in_specs=[pl.BlockSpec(memory_space=pltpu.SMEM)] + [vmem] * 6,
+        in_specs=[pl.BlockSpec(memory_space=pltpu.SMEM)] + [vmem] * 8,
         out_specs=(vmem, vmem),
-        scratch_shapes=[pltpu.VMEM((rows, 128), BF16), pltpu.VMEM((8, rows), F32)],
-        name="predict",
-    )(bucket_counts, here, there, cells, fractions, observed, chan_weights[None, :])
+        scratch_shapes=[pltpu.VMEM((8, rows), F32)],
+        name="predict_second",
+        compiler_params=LIMIT,
+    )(
+        bucket_counts, there, factors, cos_sum, sin_sum,
+        cells, fractions, observed, chan_weights[None, :],
+    )
     got = lax.all_to_all(packed, TILE, 0, 0, tiled=True)
     share = BAND // owners
     partial = pl.pallas_call(
@@ -214,6 +240,7 @@
         out_specs=vmem,
         scratch_shapes=[pltpu.VMEM((2 * BAND, width), F32)],
         name="gridding",
+        compiler_params=LIMIT,
     )(got)
     parts = lax.all_to_all(partial, VIS, 0, 0, tiled=True)
     total = jnp.sum(parts.astype(F32), axis=0)

time: 84.7 us -> 78.9 us (0.932)
  blocking collectives: 61.7 us -> 50.5 us
  starting transfers between devices: 0.01 us -> 4.54 us
  waiting for transfers between devices: 1.53 us -> 4.79 us
  Pallas kernels: 17.3 us -> 15.1 us
    all_to_all x1, blocking collectives: 29 us -> 20.2 us  [on_device(): lax.all_to_all(jnp.broadcast_to(mine[None], (members,) + mine.shape), pla...]
    ppermute x1 -> x4, starting transfers between devices: 0.01 us -> 4.54 us  [the longest x3 4.44 us: on_device(): lax.ppermute(own, 'vis_0', [(k, (k + step) % line) for k in range(line)])]
    ppermute x1 -> x4, waiting for transfers between devices: 1.53 us -> 4.79 us  [the longest x3 4.78 us: on_device(): lax.ppermute(own, 'vis_0', [(k, (k + step) % line) for k in range(line)])]
    pallas_call x1, Pallas kernels: 8.86 us -> 7.15 us  [on_device(): pl.pallas_call(grid_kernel, out_shape=jax.ShapeDtypeStruct((owners, 2 * s...]
    all_to_all x1, blocking collectives: 10.1 us -> 8.5 us  [on_device(): got = lax.all_to_all(packed, TILE, 0, 0, tiled=True)]
    pallas_call x1 -> x2, Pallas kernels: 8.43 us -> 7.91 us  [the longest x1 4.52 us: on_device(): pl.pallas_call(second_kernel, out_shape=(jax.ShapeDtypeStruct(observed.sh...]
  transfers between devices with their start and end apart: 1 -> 4, of which waited for: 1 -> 3; matrix products, arithmetic and copies ran while one was open for 0% -> 0% of each run, Pallas kernels for 0% -> 4%
where the time goes in v3:
time: 78.9 us; the launch traced here: 78.7 us
  blocking collectives  50.5 us (64%)
  Pallas kernels  15.1 us (19%)
  waiting for transfers between devices  4.79 us (6%)
  starting transfers between devices  4.54 us (6%)
  local copies, waits for them, and re-layouts  2.31 us (3%)
  other arithmetic  0.8 us (1%)
    all_to_all x1, blocking collectives, on_device(): parts = lax.all_to_all(partial, VIS, 0, 0, tiled=True)  21.8 us
    all_to_all x1, blocking collectives, on_device(): lax.all_to_all(jnp.broadcast_to(mine[None], (members,) + mine.shape), pla...  20.2 us
    all_to_all x1, blocking collectives, on_device(): got = lax.all_to_all(packed, TILE, 0, 0, tiled=True)  8.5 us
    pallas_call x1, Pallas kernels, on_device(): pl.pallas_call(grid_kernel, out_shape=jax.ShapeDtypeStruct((owners, 2 * s...  7.15 us
    ppermute x3, waiting for transfers between devices, on_device(): lax.ppermute(own, 'vis_0', [(k, (k + step) % line) for k in range(line)])  4.78 us
    pallas_call x1, Pallas kernels, on_device(): pl.pallas_call(second_kernel, out_shape=(jax.ShapeDtypeStruct(observed.sh...  4.52 us
    ppermute x3, starting transfers between devices, on_device(): lax.ppermute(own, 'vis_0', [(k, (k + step) % line) for k in range(line)])  4.44 us
    pallas_call x1, Pallas kernels, on_device(): pl.pallas_call(first_kernel, out_shape=(jax.ShapeDtypeStruct((rows, 128),...  3.38 us
  transfers between devices with their start and end apart: 4, of which 3 were waited for; matrix products, arithmetic and copies ran while one was open for 0% of the time, Pallas kernels for 4%

profile of v3, /device:TPU:32, one launch (start us, length us, event | category | flops | bytes accessed | tf_op | source)
XLA Modules:
  0.0 78.7 jit_solution(9618014232712286963)
XLA Ops:
  0.6 0.7 and_add_fusion
  1.3 0.1 broadcast_in_dim.44
  1.4 0.1 broadcast_in_dim.40
  1.5 0.1 broadcast_in_dim.38
  1.5 0.0 copy-start.5
  1.5 0.1 broadcast_in_dim.42
  1.6 0.6 copy-done.5
  2.2 0.1 concatenate.9
  2.3 20.2 %all_to_all.15 = bf16[32,8,128]{2,1,0:T(8,128)(2,1)S(1)} all-to-all(bf16[32,8,128]{2,1,0:T(8,128)(2,1)S(1)} %broadcast_in_dim.45), channel_id=1, replica_groups=mesh['vis_0'=4,'vis_1'=8,'tile_0'=4,'tile_1'=2] {'vis_1','tile_0'}, dimensions={0} | all-to-all | bytes 131072 | tf_op jit(solution)/shard_map/all_to_all | solution.py:200
  22.5 0.0 copy-start.1
  22.5 0.0 copy-start.2
  22.5 2.8 %collective-permute-start.2 = (bf16[256,128]{1,0:T(8,128)(2,1)S(1)}, bf16[256,128]{1,0:T(8,128)(2,1)S(1)}, u32[]{:S(2)}, u32[]{:S(2)}) collective-permute-start(bf16[256,128]{1,0:T(8,128)(2,1)S(1)} %bitcast.12), channel_id=1, source_target_pairs={{0,192},{64,0},{128,64},{192,128},{1,193},{65,1},{129,65},{193,129... | collective-permute-start | bytes 196616 | tf_op jit(solution)/shard_map/ppermute | solution.py:205
  25.3 0.8 %collective-permute-start.1 = (bf16[256,128]{1,0:T(8,128)(2,1)S(1)}, bf16[256,128]{1,0:T(8,128)(2,1)S(1)}, u32[]{:S(2)}, u32[]{:S(2)}) collective-permute-start(bf16[256,128]{1,0:T(8,128)(2,1)S(1)} %bitcast.13), channel_id=1, source_target_pairs={{0,128},{64,192},{128,0},{192,64},{1,129},{65,193},{129,1},{193,65... | collective-permute-start | bytes 196616 | tf_op jit(solution)/shard_map/ppermute | solution.py:205
  26.1 0.9 %collective-permute-start = (bf16[256,128]{1,0:T(8,128)(2,1)S(1)}, bf16[256,128]{1,0:T(8,128)(2,1)S(1)}, u32[]{:S(2)}, u32[]{:S(2)}) collective-permute-start(bf16[256,128]{1,0:T(8,128)(2,1)S(1)} %bitcast.14), channel_id=1, source_target_pairs={{0,64},{64,128},{128,192},{192,0},{1,65},{65,129},{129,193},{193,1... | collective-permute-start | bytes 196616 | tf_op jit(solution)/shard_map/ppermute | solution.py:205
  27.0 0.2 collective-permute-done.2.refs_3_
  27.2 3.9 %collective-permute-done.1.refs_2_ = bf16[256,128]{1,0:T(8,128)(2,1)S(1)} collective-permute-done((bf16[256,128]{1,0:T(8,128)(2,1)S(1)}, bf16[256,128]{1,0:T(8,128)(2,1)S(1)}, u32[]{:S(2)}, u32[]{:S(2)}) %collective-permute-start.1) | collective-permute-done | bytes 65568 | tf_op jit(solution)/shard_map/ppermute | solution.py:205
  31.1 0.7 collective-permute-done.refs_1_
  31.8 0.0 copy-start
  31.8 0.1 collective-permute-start.3
  31.9 0.0 copy-done.1
  31.9 0.0 copy-done.2
  31.9 3.4 %predict_first.1 = (bf16[1024,128]{1,0:T(8,128)(2,1)S(1)}, f32[1024,128]{1,0:T(8,128)S(1)}, f32[1024,128]{1,0:T(8,128)S(1)}) custom-call(bf16[256,128]{1,0:T(8,128)(2,1)S(1)} %bitcast.16, bf16[256,128]{1,0:T(8,128)(2,1)S(1)} %collective-permute-done.refs_1_, bf16[256,128]{1,0:T(8,128)(2,1)S(1)} %collective-permute-done.1.refs_2_, ...), custom_call_target="tpu_custom_call" | custom-call | tf_op jit(solution)/shard_map/predict_first/pallas_call | solution.py:211
  35.3 0.0 collective-permute-done.3.comps
  35.3 0.0 copy-start.3
  35.3 0.0 copy-start.4
  35.3 0.0 copy-done
  35.3 0.6 copy-done.3
  36.0 0.0 copy-done.4
  36.0 4.5 %predict_second.1 = (bf16[1024,128]{1,0:T(8,128)(2,1)}, f32[8,8,512]{2,1,0:T(8,128)S(1)}) custom-call(s32[1,8]{1,0:T(1,128)S(1)} %copy-done.3, bf16[1024,128]{1,0:T(8,128)(2,1)S(1)} %collective-permute-done.3.comps, bf16[1024,128]{1,0:T(8,128)(2,1)S(1)} %get-tuple-element.7.factors, f32[1024,128]{1,0:T(8,128)S(1)} %get-tuple-element.8.cos_in, ...), custom_call_target="tpu_custom_call" | custom-call | tf_op jit(solution)/shard_map/predict_second/pallas_call | solution.py:219
  40.5 8.5 %all_to_all.16.got = f32[8,8,512]{2,1,0:T(8,128)S(1)} all-to-all(f32[8,8,512]{2,1,0:T(8,128)S(1)} %get-tuple-element.11), channel_id=1, replica_groups=mesh['vis_0'=4,'vis_1'=8,'tile_0'=4,'tile_1'=2] {'tile_0','tile_1'}, dimensions={0} | all-to-all | bytes 262144 | tf_op jit(solution)/shard_map/all_to_all | solution.py:234
  49.0 7.2 %gridding.1 = bf16[32,8,1024]{2,1,0:T(8,128)(2,1)S(1)} custom-call(f32[8,8,512]{2,1,0:T(8,128)S(1)} %all_to_all.16.got), custom_call_target="tpu_custom_call" | custom-call | tf_op jit(solution)/shard_map/gridding/pallas_call | solution.py:236
  56.2 21.8 %all_to_all.17 = bf16[32,8,1024]{2,1,0:T(8,128)(2,1)S(1)} all-to-all(bf16[32,8,1024]{2,1,0:T(8,128)(2,1)S(1)} %gridding.1), channel_id=1, replica_groups=mesh['vis_0'=4,'vis_1'=8,'tile_0'=4,'tile_1'=2] {'vis_0','vis_1'}, dimensions={0} | all-to-all | bytes 1048576 | tf_op jit(solution)/shard_map/all_to_all | solution.py:245
  78.0 0.1 convert_reduce_fusion
  78.0 0.6 reshape.12
  (4 shorter events, 0.0 us)
Async XLA Ops:
  1.5 0.7 copy-start.5
  22.5 9.4 %copy-start.1 = (s32[2,1024]{1,0:T(2,128)S(1)}, s32[2,1024]{1,0:T(2,128)}, u32[]{:S(2)}) copy-start(s32[2,1024]{1,0:T(2,128)} %cells.1) | copy-start | bytes 24580
  22.5 9.4 %copy-start.2 = (f32[2,1024]{1,0:T(2,128)S(1)}, f32[2,1024]{1,0:T(2,128)}, u32[]{:S(2)}) copy-start(f32[2,1024]{1,0:T(2,128)} %fractions.1) | copy-start | bytes 24580
  22.5 4.7 %collective-permute-start.2 = (bf16[256,128]{1,0:T(8,128)(2,1)S(1)}, bf16[256,128]{1,0:T(8,128)(2,1)S(1)}, u32[]{:S(2)}, u32[]{:S(2)}) collective-permute-start(bf16[256,128]{1,0:T(8,128)(2,1)S(1)} %bitcast.12), channel_id=1, source_target_pairs={{0,192},{64,0},{128,64},{192,128},{1,193},{65,1},{129,65},{193,129... | collective-permute-start | bytes 196616 | tf_op jit(solution)/shard_map/ppermute | solution.py:205
  25.3 5.8 %collective-permute-start.1 = (bf16[256,128]{1,0:T(8,128)(2,1)S(1)}, bf16[256,128]{1,0:T(8,128)(2,1)S(1)}, u32[]{:S(2)}, u32[]{:S(2)}) collective-permute-start(bf16[256,128]{1,0:T(8,128)(2,1)S(1)} %bitcast.13), channel_id=1, source_target_pairs={{0,128},{64,192},{128,0},{192,64},{1,129},{65,193},{129,1},{193,65... | collective-permute-start | bytes 196616 | tf_op jit(solution)/shard_map/ppermute | solution.py:205
  26.1 5.7 %collective-permute-start = (bf16[256,128]{1,0:T(8,128)(2,1)S(1)}, bf16[256,128]{1,0:T(8,128)(2,1)S(1)}, u32[]{:S(2)}, u32[]{:S(2)}) collective-permute-start(bf16[256,128]{1,0:T(8,128)(2,1)S(1)} %bitcast.14), channel_id=1, source_target_pairs={{0,64},{64,128},{128,192},{192,0},{1,65},{65,129},{129,193},{193,1... | collective-permute-start | bytes 196616 | tf_op jit(solution)/shard_map/ppermute | solution.py:205
  31.8 3.6 %copy-start = (bf16[1024,128]{1,0:T(8,128)(2,1)S(1)}, bf16[1024,128]{1,0:T(8,128)(2,1)}, u32[]{:S(2)}) copy-start(bf16[1024,128]{1,0:T(8,128)(2,1)} %observed.1) | copy-start | bytes 786436
  31.8 3.5 %collective-permute-start.3 = (bf16[1024,128]{1,0:T(8,128)(2,1)S(1)}, bf16[1024,128]{1,0:T(8,128)(2,1)S(1)}, u32[]{:S(2)}, u32[]{:S(2)}) collective-permute-start(bf16[1024,128]{1,0:T(8,128)(2,1)S(1)} %pad_maximum_fusion), channel_id=1, source_target_pairs={{0,1},{1,0},{2,3},{3,2},{4,5},{5,4},{6,7},{7,6},{8,9},{9,8},{10,11... | collective-permute-start | bytes 786440 | tf_op jit(solution)/shard_map/ppermute | solution.py:208
  35.3 0.7 copy-start.3
  35.3 0.7 copy-start.4

commit v4 on v3

--- a/solution.py
+++ b/solution.py
@@ -109,8 +109,7 @@
     counts, comps, factors, cos_in, sin_in, cells, fractions, observed, weights, residual, packed, fields
 ):
     rows = observed.shape[0]
-    slot = packed.shape[2]
-    tiles = packed.shape[0]
+    owners, tiles, _, slot = packed.shape
     start = []
     total = counts[0, 0] * 0
     for t in range(tiles):
@@ -135,56 +134,64 @@
     sums = lax.dot_general(w_rows, res, NT, preferred_element_type=F32)
     fields[0:1, :] = sums[0:1] + sums[1:2] + sums[2:3]
     fields[1:2, :] = sums[3:4] + sums[4:5] + sums[5:6]
-    fields[2:4, :] = fractions[...]
-    fields[4:6, :] = cells[...].astype(F32)
-    fields[6:8, :] = jnp.zeros((2, rows), F32)
+    fields[2:4, :] = cells[...].astype(F32) + 0.5 * fractions[...]
+    fields[4:8, :] = jnp.zeros((4, rows), F32)
     everything = fields[...]
-    row_of = lax.broadcasted_iota(jnp.int32, (8, slot), 0)
-    place = lax.broadcasted_iota(jnp.int32, (8, slot), 1)
+    row_of = lax.broadcasted_iota(jnp.int32, (4, slot), 0)
+    place = lax.broadcasted_iota(jnp.int32, (4, slot), 1)
     for t in range(tiles):
-        moved = pltpu.roll(everything, (rows - start[t]) & (rows - 1), 1)[:, :slot]
+        moved = pltpu.roll(everything, (rows - start[t]) & (rows - 1), 1)[:4, :slot]
         moved = jnp.where((row_of >= 2) | (place < counts[0, t]), moved, 0.0)
-        base = float(t * (GRID // tiles))
-        packed[t] = moved - jnp.where(row_of == 4, base, 0.0)
+        for owner in range(owners):
+            base = float((t * owners + owner) * (GRID // (tiles * owners)))
+            packed[owner, t] = moved - jnp.where(row_of == 2, base, 0.0)
 
 
 def grid_kernel(got, out, acc):
     sources, _, slot = got.shape
-    slot = slot * 4
-    sources = sources // 4
-    width = acc.shape[1]
-    high = acc.shape[0]
+    group = 8
+    count = group * slot
+    width = out.shape[2]
     scale = -0.7213475204444817
+    first_line = lax.broadcasted_iota(jnp.int32, (BAND, count), 0)
+    line_float = first_line.astype(F32)
+    column = lax.broadcasted_iota(jnp.int32, (width, count), 0)
+    column_float = column.astype(F32)
     acc[...] = jnp.zeros(acc.shape, F32)
-    line = lax.broadcasted_iota(jnp.int32, (high, slot), 0)
-    line_row = line >> 1
-    line_float = line_row.astype(F32)
-    imag = (line & 1) == 1
-    block = 128
-    column = lax.broadcasted_iota(jnp.int32, (block, width), 1)
-    column_float = column.astype(F32)
-
-    def source_step(step, carry):
-        data = jnp.concatenate([got[step * 4 + k] for k in range(4)], axis=1)
-        value = jnp.where(imag, data[1:2, :], data[0:1, :])
-        off = line_float - (data[5:6, :] + 3.0 + data[3:4, :])
-        kernel = jnp.exp2(off * off * scale)
-        near = (lambda t: t.astype(jnp.uint32) < 8)(line_row - data[5:6, :].astype(jnp.int32))
-        left = jnp.where(near, value * kernel, 0.0).astype(BF16)
-        turned = jnp.concatenate([data[4:5], data[4:5] + 3.0 + data[2:3], data[:6]]).T
-        cols = []
-        for r in range(slot // block):
-            sub = turned[r * block : (r + 1) * block]
-            first_col = sub[:, 0:1].astype(jnp.int32)
-            off_u = column_float - sub[:, 1:2]
-            weight = jnp.exp2(off_u * off_u * scale)
-            cols.append(jnp.where((lambda t: t.astype(jnp.uint32) < 8)(column - first_col), weight, 0.0).astype(BF16))
-        spread = jnp.concatenate(cols)
-        acc[...] += lax.dot_general(left, spread, NN, preferred_element_type=F32)
+
+    def step(number, carry):
+        data = jnp.concatenate([got[number * group + k] for k in range(group)], axis=1)
+        row_start = jnp.floor(data[3:4])
+        row_centre = 3.0 - row_start + 2.0 * data[3:4]
+        off = line_float - row_centre
+        near = (first_line - row_start.astype(jnp.int32)).astype(jnp.uint32) < 8
+        kernel = jnp.where(near, jnp.exp2(off * off * scale), 0.0)
+        left = jnp.concatenate([(data[0:1] * kernel).astype(BF16), (data[1:2] * kernel).astype(BF16)])
+        col_start = jnp.floor(data[2:3])
+        col_centre = 3.0 - col_start + 2.0 * data[2:3]
+        off_u = column_float - col_centre
+        near_u = (column - col_start.astype(jnp.int32)).astype(jnp.uint32) < 8
+        spread = jnp.where(near_u, jnp.exp2(off_u * off_u * scale), 0.0).astype(BF16)
+        acc[...] += lax.dot_general(left, spread, NT, preferred_element_type=F32)
         return carry
 
-    lax.fori_loop(0, sources, source_step, 0)
-    out[...] = acc[...].astype(BF16).reshape(out.shape)
+    lax.fori_loop(0, sources // group, step, 0)
+    upper = lax.broadcasted_iota(jnp.int32, (8, width), 0) < 4
+    for g in range(BAND // 8):
+        real = acc[8 * g : 8 * g + 8]
+        imag = acc[BAND + 8 * g : BAND + 8 * g + 8]
+        out[2 * g] = jnp.where(upper, real, pltpu.roll(imag, 4, 0)).astype(BF16)
+        out[2 * g + 1] = jnp.where(upper, pltpu.roll(real, 4, 0), imag).astype(BF16)
+
+
+def sum_kernel(got, out):
+    blocks, sources, lines, width = got.shape
+    share = lines // 2
+    for b in range(blocks):
+        total = jnp.sum(got[b].astype(F32), axis=0)
+        for c in range(2):
+            for j in range(share):
+                out[j, c : c + 1, b * width : (b + 1) * width] = total[c * share + j : c * share + j + 1]
 
 
 def on_device(spectra, positions, observed, cells, fractions, bucket_counts, chan_weights):
@@ -220,7 +227,7 @@
         second_kernel,
         out_shape=(
             jax.ShapeDtypeStruct(observed.shape, BF16),
-            jax.ShapeDtypeStruct((tiles, 8, slot), F32),
+            jax.ShapeDtypeStruct((line, tiles, 4, slot), F32),
         ),
         in_specs=[pl.BlockSpec(memory_space=pltpu.SMEM)] + [vmem] * 8,
         out_specs=(vmem, vmem),
@@ -231,20 +238,30 @@
         bucket_counts, there, factors, cos_sum, sin_sum,
         cells, fractions, observed, chan_weights[None, :],
     )
-    got = lax.all_to_all(packed, TILE, 0, 0, tiled=True)
+    got = lax.all_to_all(
+        packed.reshape(line * tiles, 4, slot), ("vis_0",) + TILE, 0, 0, tiled=True
+    )
     share = BAND // owners
+    block = width // line
     partial = pl.pallas_call(
         grid_kernel,
-        out_shape=jax.ShapeDtypeStruct((owners, 2 * share, width), BF16),
+        out_shape=jax.ShapeDtypeStruct((owners, 2 * share, block), BF16),
         in_specs=[vmem],
         out_specs=vmem,
-        scratch_shapes=[pltpu.VMEM((2 * BAND, width), F32)],
+        scratch_shapes=[pltpu.VMEM((2 * BAND, block), F32)],
         name="gridding",
         compiler_params=LIMIT,
     )(got)
     parts = lax.all_to_all(partial, VIS, 0, 0, tiled=True)
-    total = jnp.sum(parts.astype(F32), axis=0)
-    return residual, total.reshape(share, 2, width)
+    total = pl.pallas_call(
+        sum_kernel,
+        out_shape=jax.ShapeDtypeStruct((share, 2, width), F32),
+        in_specs=[vmem],
+        out_specs=vmem,
+        name="add_shares",
+        compiler_params=LIMIT,
+    )(parts.reshape(line, owners // line, 2 * share, block))
+    return residual, total
 
 
 def solution(mesh):

time: 78.9 us -> 76.4 us (0.968)
  blocking collectives: 50.5 us -> 47.2 us
  Pallas kernels: 15.1 us -> 16.5 us
    all_to_all x1, blocking collectives: 21.8 us -> 14.6 us  [on_device(): parts = lax.all_to_all(partial, VIS, 0, 0, tiled=True)]
    all_to_all x1, blocking collectives: 8.5 us -> 12.5 us  [on_device(): lax.all_to_all(packed.reshape(line * tiles, 4, slot), ('vis_0',) + TILE,...]
where the time goes in v4:
time: 76.4 us; the launch traced here: 76.1 us
  blocking collectives  47.2 us (62%)
  Pallas kernels  16.5 us (22%)
  waiting for transfers between devices  4.79 us (6%)
  starting transfers between devices  4.54 us (6%)
  local copies, waits for them, and re-layouts  1.67 us (2%)
    all_to_all x1, blocking collectives, on_device(): lax.all_to_all(jnp.broadcast_to(mine[None], (members,) + mine.shape), pla...  20.2 us
    all_to_all x1, blocking collectives, on_device(): parts = lax.all_to_all(partial, VIS, 0, 0, tiled=True)  14.6 us
    all_to_all x1, blocking collectives, on_device(): lax.all_to_all(packed.reshape(line * tiles, 4, slot), ('vis_0',) + TILE,...  12.5 us
    pallas_call x1, Pallas kernels, on_device(): pl.pallas_call(grid_kernel, out_shape=jax.ShapeDtypeStruct((owners, 2 * s...  7.9 us
    ppermute x3, waiting for transfers between devices, on_device(): lax.ppermute(own, 'vis_0', [(k, (k + step) % line) for k in range(line)])  4.78 us
    pallas_call x1, Pallas kernels, on_device(): pl.pallas_call(second_kernel, out_shape=(jax.ShapeDtypeStruct(observed.sh...  4.52 us
    ppermute x3, starting transfers between devices, on_device(): lax.ppermute(own, 'vis_0', [(k, (k + step) % line) for k in range(line)])  4.44 us
    pallas_call x1, Pallas kernels, on_device(): pl.pallas_call(first_kernel, out_shape=(jax.ShapeDtypeStruct((rows, 128),...  3.38 us
  transfers between devices with their start and end apart: 4, of which 3 were waited for; matrix products, arithmetic and copies ran while one was open for 0% of the time, Pallas kernels for 4%

profile of v4, /device:TPU:32, one launch (start us, length us, event | category | flops | bytes accessed | tf_op | source)
XLA Modules:
  0.0 76.1 jit_solution(15983012333065153027)
XLA Ops:
  0.6 0.7 and_add_fusion
  1.3 0.1 broadcast_in_dim.44
  1.4 0.1 broadcast_in_dim.40
  1.5 0.1 broadcast_in_dim.38
  1.5 0.0 copy-start.5
  1.5 0.1 broadcast_in_dim.42
  1.6 0.6 copy-done.5
  2.2 0.1 concatenate.9
  2.3 20.2 %all_to_all.15 = bf16[32,8,128]{2,1,0:T(8,128)(2,1)S(1)} all-to-all(bf16[32,8,128]{2,1,0:T(8,128)(2,1)S(1)} %broadcast_in_dim.45), channel_id=1, replica_groups=mesh['vis_0'=4,'vis_1'=8,'tile_0'=4,'tile_1'=2] {'vis_1','tile_0'}, dimensions={0} | all-to-all | bytes 131072 | tf_op jit(solution)/shard_map/all_to_all | solution.py:207
  22.5 0.0 copy-start.1
  22.5 0.0 copy-start.2
  22.5 2.8 %collective-permute-start.2 = (bf16[256,128]{1,0:T(8,128)(2,1)S(1)}, bf16[256,128]{1,0:T(8,128)(2,1)S(1)}, u32[]{:S(2)}, u32[]{:S(2)}) collective-permute-start(bf16[256,128]{1,0:T(8,128)(2,1)S(1)} %bitcast.14), channel_id=1, source_target_pairs={{0,192},{64,0},{128,64},{192,128},{1,193},{65,1},{129,65},{193,129... | collective-permute-start | bytes 196616 | tf_op jit(solution)/shard_map/ppermute | solution.py:212
  25.3 0.8 %collective-permute-start.1 = (bf16[256,128]{1,0:T(8,128)(2,1)S(1)}, bf16[256,128]{1,0:T(8,128)(2,1)S(1)}, u32[]{:S(2)}, u32[]{:S(2)}) collective-permute-start(bf16[256,128]{1,0:T(8,128)(2,1)S(1)} %bitcast.15), channel_id=1, source_target_pairs={{0,128},{64,192},{128,0},{192,64},{1,129},{65,193},{129,1},{193,65... | collective-permute-start | bytes 196616 | tf_op jit(solution)/shard_map/ppermute | solution.py:212
  26.1 0.9 %collective-permute-start = (bf16[256,128]{1,0:T(8,128)(2,1)S(1)}, bf16[256,128]{1,0:T(8,128)(2,1)S(1)}, u32[]{:S(2)}, u32[]{:S(2)}) collective-permute-start(bf16[256,128]{1,0:T(8,128)(2,1)S(1)} %bitcast.16), channel_id=1, source_target_pairs={{0,64},{64,128},{128,192},{192,0},{1,65},{65,129},{129,193},{193,1... | collective-permute-start | bytes 196616 | tf_op jit(solution)/shard_map/ppermute | solution.py:212
  27.0 0.2 collective-permute-done.2.refs_3_
  27.2 3.9 %collective-permute-done.1.refs_2_ = bf16[256,128]{1,0:T(8,128)(2,1)S(1)} collective-permute-done((bf16[256,128]{1,0:T(8,128)(2,1)S(1)}, bf16[256,128]{1,0:T(8,128)(2,1)S(1)}, u32[]{:S(2)}, u32[]{:S(2)}) %collective-permute-start.1) | collective-permute-done | bytes 65568 | tf_op jit(solution)/shard_map/ppermute | solution.py:212
  31.1 0.7 collective-permute-done.refs_1_
  31.8 0.0 copy-start
  31.8 0.1 collective-permute-start.3
  31.9 0.0 copy-done.1
  31.9 0.0 copy-done.2
  31.9 3.4 %predict_first.1 = (bf16[1024,128]{1,0:T(8,128)(2,1)S(1)}, f32[1024,128]{1,0:T(8,128)S(1)}, f32[1024,128]{1,0:T(8,128)S(1)}) custom-call(bf16[256,128]{1,0:T(8,128)(2,1)S(1)} %bitcast.18, bf16[256,128]{1,0:T(8,128)(2,1)S(1)} %collective-permute-done.refs_1_, bf16[256,128]{1,0:T(8,128)(2,1)S(1)} %collective-permute-done.1.refs_2_, ...), custom_call_target="tpu_custom_call" | custom-call | tf_op jit(solution)/shard_map/predict_first/pallas_call | solution.py:218
  35.3 0.0 collective-permute-done.3.comps
  35.3 0.0 copy-start.3
  35.3 0.0 copy-start.4
  35.3 0.0 copy-done
  35.3 0.6 copy-done.3
  36.0 0.0 copy-done.4
  36.0 4.5 %predict_second.1 = (bf16[1024,128]{1,0:T(8,128)(2,1)}, f32[4,8,4,512]{3,2,1,0:T(4,128)S(1)}) custom-call(s32[1,8]{1,0:T(1,128)S(1)} %copy-done.3, bf16[1024,128]{1,0:T(8,128)(2,1)S(1)} %collective-permute-done.3.comps, bf16[1024,128]{1,0:T(8,128)(2,1)S(1)} %get-tuple-element.7.factors, f32[1024,128]{1,0:T(8,128)S(1)} %get-tuple-element.8.cos_in, ...), custom_call_target="tpu_custom_call" | custom-call | tf_op jit(solution)/shard_map/predict_second/pallas_call | solution.py:226
  40.5 12.5 %all_to_all.16.got = f32[32,4,512]{2,1,0:T(4,128)S(1)} all-to-all(f32[32,4,512]{2,1,0:T(4,128)S(1)} %bitcast.20), channel_id=1, replica_groups=mesh['vis_0'=4,'vis_1'=8,'tile_0'=4,'tile_1'=2] {'vis_0','tile_0','tile_1'}, dimensions={0} | all-to-all | bytes 524288 | tf_op jit(solution)/shard_map/all_to_all | solution.py:241
  53.0 7.9 %gridding.1 = bf16[32,8,256]{2,1,0:T(8,128)(2,1)S(1)} custom-call(f32[32,4,512]{2,1,0:T(4,128)S(1)} %all_to_all.16.got), custom_call_target="tpu_custom_call" | custom-call | tf_op jit(solution)/shard_map/gridding/pallas_call | solution.py:246
  60.9 14.6 %all_to_all.17 = bf16[32,8,256]{2,1,0:T(8,128)(2,1)S(1)} all-to-all(bf16[32,8,256]{2,1,0:T(8,128)(2,1)S(1)} %gridding.1), channel_id=1, replica_groups=mesh['vis_0'=4,'vis_1'=8,'tile_0'=4,'tile_1'=2] {'vis_0','vis_1'}, dimensions={0} | all-to-all | bytes 262144 | tf_op jit(solution)/shard_map/all_to_all | solution.py:255
  75.5 0.6 add_shares.1
  (4 shorter events, 0.0 us)
Async XLA Ops:
  1.5 0.7 copy-start.5
  22.5 9.4 %copy-start.1 = (s32[2,1024]{1,0:T(2,128)S(1)}, s32[2,1024]{1,0:T(2,128)}, u32[]{:S(2)}) copy-start(s32[2,1024]{1,0:T(2,128)} %cells.1) | copy-start | bytes 24580
  22.5 9.4 %copy-start.2 = (f32[2,1024]{1,0:T(2,128)S(1)}, f32[2,1024]{1,0:T(2,128)}, u32[]{:S(2)}) copy-start(f32[2,1024]{1,0:T(2,128)} %fractions.1) | copy-start | bytes 24580
  22.5 4.7 %collective-permute-start.2 = (bf16[256,128]{1,0:T(8,128)(2,1)S(1)}, bf16[256,128]{1,0:T(8,128)(2,1)S(1)}, u32[]{:S(2)}, u32[]{:S(2)}) collective-permute-start(bf16[256,128]{1,0:T(8,128)(2,1)S(1)} %bitcast.14), channel_id=1, source_target_pairs={{0,192},{64,0},{128,64},{192,128},{1,193},{65,1},{129,65},{193,129... | collective-permute-start | bytes 196616 | tf_op jit(solution)/shard_map/ppermute | solution.py:212
  25.3 5.8 %collective-permute-start.1 = (bf16[256,128]{1,0:T(8,128)(2,1)S(1)}, bf16[256,128]{1,0:T(8,128)(2,1)S(1)}, u32[]{:S(2)}, u32[]{:S(2)}) collective-permute-start(bf16[256,128]{1,0:T(8,128)(2,1)S(1)} %bitcast.15), channel_id=1, source_target_pairs={{0,128},{64,192},{128,0},{192,64},{1,129},{65,193},{129,1},{193,65... | collective-permute-start | bytes 196616 | tf_op jit(solution)/shard_map/ppermute | solution.py:212
  26.1 5.7 %collective-permute-start = (bf16[256,128]{1,0:T(8,128)(2,1)S(1)}, bf16[256,128]{1,0:T(8,128)(2,1)S(1)}, u32[]{:S(2)}, u32[]{:S(2)}) collective-permute-start(bf16[256,128]{1,0:T(8,128)(2,1)S(1)} %bitcast.16), channel_id=1, source_target_pairs={{0,64},{64,128},{128,192},{192,0},{1,65},{65,129},{129,193},{193,1... | collective-permute-start | bytes 196616 | tf_op jit(solution)/shard_map/ppermute | solution.py:212
  31.8 3.6 %copy-start = (bf16[1024,128]{1,0:T(8,128)(2,1)S(1)}, bf16[1024,128]{1,0:T(8,128)(2,1)}, u32[]{:S(2)}) copy-start(bf16[1024,128]{1,0:T(8,128)(2,1)} %observed.1) | copy-start | bytes 786436
  31.8 3.5 %collective-permute-start.3 = (bf16[1024,128]{1,0:T(8,128)(2,1)S(1)}, bf16[1024,128]{1,0:T(8,128)(2,1)S(1)}, u32[]{:S(2)}, u32[]{:S(2)}) collective-permute-start(bf16[1024,128]{1,0:T(8,128)(2,1)S(1)} %pad_maximum_fusion), channel_id=1, source_target_pairs={{0,1},{1,0},{2,3},{3,2},{4,5},{5,4},{6,7},{7,6},{8,9},{9,8},{10,11... | collective-permute-start | bytes 786440 | tf_op jit(solution)/shard_map/ppermute | solution.py:215
  35.3 0.7 copy-start.3
  35.3 0.7 copy-start.4

commit v5 on v4

--- a/solution.py
+++ b/solution.py
@@ -31,17 +31,20 @@
     return [first, second, rest - second]
 
 
-def component_rows(spectra, positions):
-    low = ((positions + 64) & 127) - 64
-    high = (positions - low) >> 7
+def component_kernel(spectra, positions, out):
+    count, channels = spectra.shape
+    pixels = positions[...]
+    low = ((pixels + 64) & 127) - 64
+    high = (pixels - low) >> 7
     digits = jnp.concatenate(
-        [
-            jnp.broadcast_to(d[None], (n, d.shape[0]))
-            for d, n in ((high[0], 4), (low[0], 5), (high[1], 4), (low[1], 5))
-        ]
-    ).astype(BF16)
-    rows = jnp.concatenate([spectra, digits])
-    return jnp.pad(rows, ((0, 128 - rows.shape[0]), (0, 0))).T
+        [high[0:1]] * 4 + [low[0:1]] * 5 + [high[1:2]] * 4 + [low[1:2]] * 5 + [high[0:1] * 0] * 14
+    ).astype(F32)
+    blank = jnp.zeros((digits.shape[0], 128 - count), F32)
+    turned = jnp.concatenate([digits, blank], axis=1).T[:count]
+    rest = jnp.zeros((count, 128 - channels - turned.shape[1]), F32)
+    row = jnp.concatenate([spectra[...].astype(F32), turned, rest], axis=1).astype(BF16)
+    for member in range(out.shape[0]):
+        out[member] = row
 
 
 def row_factors(cells, fractions):
@@ -147,31 +150,37 @@
             packed[owner, t] = moved - jnp.where(row_of == 2, base, 0.0)
 
 
+def tap_weights(position, count):
+    start = jnp.floor(position)
+    fraction = 2.0 * (position - start)
+    first = start.astype(jnp.int32)
+    lane = lax.broadcasted_iota(jnp.int32, (8, count), 0)
+    tap = (lane - first) & 7
+    off = (tap - 3).astype(F32) - fraction
+    return jnp.exp2(off * off * -0.7213475204444817), (first + tap) >> 3
+
+
 def grid_kernel(got, out, acc):
     sources, _, slot = got.shape
-    group = 8
+    group = 16
     count = group * slot
     width = out.shape[2]
-    scale = -0.7213475204444817
-    first_line = lax.broadcasted_iota(jnp.int32, (BAND, count), 0)
-    line_float = first_line.astype(F32)
-    column = lax.broadcasted_iota(jnp.int32, (width, count), 0)
-    column_float = column.astype(F32)
     acc[...] = jnp.zeros(acc.shape, F32)
+    lines = lax.broadcasted_iota(jnp.int32, (BAND // 8, 8, count), 0)
+    columns = lax.broadcasted_iota(jnp.int32, (width // 8, 8, count), 0)
 
     def step(number, carry):
         data = jnp.concatenate([got[number * group + k] for k in range(group)], axis=1)
-        row_start = jnp.floor(data[3:4])
-        row_centre = 3.0 - row_start + 2.0 * data[3:4]
-        off = line_float - row_centre
-        near = (first_line - row_start.astype(jnp.int32)).astype(jnp.uint32) < 8
-        kernel = jnp.where(near, jnp.exp2(off * off * scale), 0.0)
-        left = jnp.concatenate([(data[0:1] * kernel).astype(BF16), (data[1:2] * kernel).astype(BF16)])
-        col_start = jnp.floor(data[2:3])
-        col_centre = 3.0 - col_start + 2.0 * data[2:3]
-        off_u = column_float - col_centre
-        near_u = (column - col_start.astype(jnp.int32)).astype(jnp.uint32) < 8
-        spread = jnp.where(near_u, jnp.exp2(off_u * off_u * scale), 0.0).astype(BF16)
+        weight, place = tap_weights(data[3:4], count)
+        here = lines == place[None]
+        left = jnp.concatenate(
+            [
+                jnp.where(here, (weight * data[k : k + 1])[None], 0.0).astype(BF16).reshape(BAND, count)
+                for k in range(2)
+            ]
+        )
+        weight, place = tap_weights(data[2:3], count)
+        spread = jnp.where(columns == place[None], weight[None], 0.0).astype(BF16).reshape(width, count)
         acc[...] += lax.dot_general(left, spread, NT, preferred_element_type=F32)
         return carry
 
@@ -200,20 +209,25 @@
     owners = lax.axis_size(VIS)
     slot = rows // 2
     width = GRID // tiles
-    devices = tiles * owners
-    mine = component_rows(spectra, positions)
     plane = ("vis_1", "tile_0")
     members = lax.axis_size(plane)
-    own = lax.all_to_all(
-        jnp.broadcast_to(mine[None], (members,) + mine.shape), plane, 0, 0, tiled=True
-    ).reshape(members * mine.shape[0], 128)
+    count = spectra.shape[1]
+    vmem = pl.BlockSpec(memory_space=pltpu.VMEM)
+    mine = pl.pallas_call(
+        component_kernel,
+        out_shape=jax.ShapeDtypeStruct((members, count, 128), BF16),
+        in_specs=[vmem] * 2,
+        out_specs=vmem,
+        name="components",
+        compiler_params=LIMIT,
+    )(spectra.T, positions)
+    own = lax.all_to_all(mine, plane, 0, 0, tiled=True).reshape(members * count, 128)
     line = lax.axis_size("vis_0")
     here = [own] + [
         lax.ppermute(own, "vis_0", [(k, (k + step) % line) for k in range(line)])
         for step in range(1, line)
     ]
     there = lax.ppermute(jnp.concatenate(here), "tile_1", [(0, 1), (1, 0)])
-    vmem = pl.BlockSpec(memory_space=pltpu.VMEM)
     sums = jax.ShapeDtypeStruct((rows, 128), F32)
     factors, cos_sum, sin_sum = pl.pallas_call(
         first_kernel,

time: 76.4 us -> 71 us (0.929)
  Pallas kernels: 16.5 us -> 11.4 us
    pallas_call x1, Pallas kernels: 7.9 us -> 2.65 us  [on_device(): pl.pallas_call(grid_kernel, out_shape=jax.ShapeDtypeStruct((owners, 2 * s...]
    unnamed x12 -> x14, local copies, waits for them, and re-layouts: 1.27 us -> 2.01 us
  transfers between devices with their start and end apart: 4 -> 4, of which waited for: 3 -> 3; matrix products, arithmetic and copies ran while one was open for 0% -> 0% of each run, Pallas kernels for 4% -> 5%
where the time goes in v5:
time: 71 us; the launch traced here: 70.7 us
  blocking collectives  47.2 us (66%)
  Pallas kernels  11.4 us (16%)
  waiting for transfers between devices  4.79 us (7%)
  starting transfers between devices  4.54 us (6%)
  local copies, waits for them, and re-layouts  2.01 us (3%)
  between operations  0.73 us (1%)
    all_to_all x1, blocking collectives, on_device(): lax.all_to_all(mine, plane, 0, 0, tiled=True).reshape(members * count, 128)  20.2 us
    all_to_all x1, blocking collectives, on_device(): parts = lax.all_to_all(partial, VIS, 0, 0, tiled=True)  14.6 us
    all_to_all x1, blocking collectives, on_device(): lax.all_to_all(packed.reshape(line * tiles, 4, slot), ('vis_0',) + TILE,...  12.5 us
    ppermute x3, waiting for transfers between devices, on_device(): lax.ppermute(own, 'vis_0', [(k, (k + step) % line) for k in range(line)])  4.78 us
    pallas_call x1, Pallas kernels, on_device(): pl.pallas_call(second_kernel, out_shape=(jax.ShapeDtypeStruct(observed.sh...  4.52 us
    ppermute x3, starting transfers between devices, on_device(): lax.ppermute(own, 'vis_0', [(k, (k + step) % line) for k in range(line)])  4.44 us
    pallas_call x1, Pallas kernels, on_device(): pl.pallas_call(first_kernel, out_shape=(jax.ShapeDtypeStruct((rows, 128),...  3.38 us
    pallas_call x1, Pallas kernels, on_device(): pl.pallas_call(grid_kernel, out_shape=jax.ShapeDtypeStruct((owners, 2 * s...  2.65 us
  transfers between devices with their start and end apart: 4, of which 3 were waited for; matrix products, arithmetic and copies ran while one was open for 0% of the time, Pallas kernels for 5%

profile of v5, /device:TPU:32, one launch (start us, length us, event | category | flops | bytes accessed | tf_op | source)
XLA Modules:
  0.0 70.7 jit_solution(10984130345795052623)
XLA Ops:
  0.6 0.0 copy-start.4
  0.6 0.7 copy-done.4
  1.3 0.0 copy-start.3
  1.3 0.7 copy-done.3
  2.0 0.2 components.1
  2.1 20.2 %all_to_all.15 = bf16[32,8,128]{2,1,0:T(8,128)(2,1)S(1)} all-to-all(bf16[32,8,128]{2,1,0:T(8,128)(2,1)S(1)} %components.1), channel_id=1, replica_groups=mesh['vis_0'=4,'vis_1'=8,'tile_0'=4,'tile_1'=2] {'vis_1','tile_0'}, dimensions={0} | all-to-all | bytes 131072 | tf_op jit(solution)/shard_map/all_to_all | solution.py:224
  22.3 0.0 copy-start.1
  22.3 0.0 copy-start.2
  22.3 2.8 %collective-permute-start.2 = (bf16[256,128]{1,0:T(8,128)(2,1)S(1)}, bf16[256,128]{1,0:T(8,128)(2,1)S(1)}, u32[]{:S(2)}, u32[]{:S(2)}) collective-permute-start(bf16[256,128]{1,0:T(8,128)(2,1)S(1)} %bitcast.5), channel_id=1, source_target_pairs={{0,192},{64,0},{128,64},{192,128},{1,193},{65,1},{129,65},{193,129... | collective-permute-start | bytes 196616 | tf_op jit(solution)/shard_map/ppermute | solution.py:227
  25.1 0.8 %collective-permute-start.1 = (bf16[256,128]{1,0:T(8,128)(2,1)S(1)}, bf16[256,128]{1,0:T(8,128)(2,1)S(1)}, u32[]{:S(2)}, u32[]{:S(2)}) collective-permute-start(bf16[256,128]{1,0:T(8,128)(2,1)S(1)} %bitcast.6), channel_id=1, source_target_pairs={{0,128},{64,192},{128,0},{192,64},{1,129},{65,193},{129,1},{193,65... | collective-permute-start | bytes 196616 | tf_op jit(solution)/shard_map/ppermute | solution.py:227
  25.9 0.9 %collective-permute-start = (bf16[256,128]{1,0:T(8,128)(2,1)S(1)}, bf16[256,128]{1,0:T(8,128)(2,1)S(1)}, u32[]{:S(2)}, u32[]{:S(2)}) collective-permute-start(bf16[256,128]{1,0:T(8,128)(2,1)S(1)} %bitcast.7), channel_id=1, source_target_pairs={{0,64},{64,128},{128,192},{192,0},{1,65},{65,129},{129,193},{193,1... | collective-permute-start | bytes 196616 | tf_op jit(solution)/shard_map/ppermute | solution.py:227
  26.8 0.2 collective-permute-done.2.refs_3_
  27.0 3.9 %collective-permute-done.1.refs_2_ = bf16[256,128]{1,0:T(8,128)(2,1)S(1)} collective-permute-done((bf16[256,128]{1,0:T(8,128)(2,1)S(1)}, bf16[256,128]{1,0:T(8,128)(2,1)S(1)}, u32[]{:S(2)}, u32[]{:S(2)}) %collective-permute-start.1) | collective-permute-done | bytes 65568 | tf_op jit(solution)/shard_map/ppermute | solution.py:227
  30.9 0.7 collective-permute-done.refs_1_
  31.6 0.0 copy-start
  31.6 0.1 collective-permute-start.3
  31.7 0.0 copy-done.1
  31.7 0.0 copy-done.2
  31.7 3.4 %predict_first.1 = (bf16[1024,128]{1,0:T(8,128)(2,1)S(1)}, f32[1024,128]{1,0:T(8,128)S(1)}, f32[1024,128]{1,0:T(8,128)S(1)}) custom-call(bf16[256,128]{1,0:T(8,128)(2,1)S(1)} %bitcast.9, bf16[256,128]{1,0:T(8,128)(2,1)S(1)} %collective-permute-done.refs_1_, bf16[256,128]{1,0:T(8,128)(2,1)S(1)} %collective-permute-done.1.refs_2_, ...), custom_call_target="tpu_custom_call" | custom-call | tf_op jit(solution)/shard_map/predict_first/pallas_call | solution.py:232
  35.1 0.0 collective-permute-done.3.comps
  35.1 0.0 copy-start.5
  35.1 0.0 copy-start.6
  35.1 0.0 copy-done
  35.1 0.6 copy-done.5
  35.8 0.0 copy-done.6
  35.8 4.5 %predict_second.1 = (bf16[1024,128]{1,0:T(8,128)(2,1)}, f32[4,8,4,512]{3,2,1,0:T(4,128)S(1)}) custom-call(s32[1,8]{1,0:T(1,128)S(1)} %copy-done.5, bf16[1024,128]{1,0:T(8,128)(2,1)S(1)} %collective-permute-done.3.comps, bf16[1024,128]{1,0:T(8,128)(2,1)S(1)} %get-tuple-element.7.factors, f32[1024,128]{1,0:T(8,128)S(1)} %get-tuple-element.8.cos_in, ...), custom_call_target="tpu_custom_call" | custom-call | tf_op jit(solution)/shard_map/predict_second/pallas_call | solution.py:240
  40.3 12.5 %all_to_all.16.got = f32[32,4,512]{2,1,0:T(4,128)S(1)} all-to-all(f32[32,4,512]{2,1,0:T(4,128)S(1)} %bitcast.11), channel_id=1, replica_groups=mesh['vis_0'=4,'vis_1'=8,'tile_0'=4,'tile_1'=2] {'vis_0','tile_0','tile_1'}, dimensions={0} | all-to-all | bytes 524288 | tf_op jit(solution)/shard_map/all_to_all | solution.py:255
  52.8 2.6 %gridding.1 = bf16[32,8,256]{2,1,0:T(8,128)(2,1)S(1)} custom-call(f32[32,4,512]{2,1,0:T(4,128)S(1)} %all_to_all.16.got), custom_call_target="tpu_custom_call" | custom-call | tf_op jit(solution)/shard_map/gridding/pallas_call | solution.py:260
  55.4 14.6 %all_to_all.17 = bf16[32,8,256]{2,1,0:T(8,128)(2,1)S(1)} all-to-all(bf16[32,8,256]{2,1,0:T(8,128)(2,1)S(1)} %gridding.1), channel_id=1, replica_groups=mesh['vis_0'=4,'vis_1'=8,'tile_0'=4,'tile_1'=2] {'vis_0','vis_1'}, dimensions={0} | all-to-all | bytes 262144 | tf_op jit(solution)/shard_map/all_to_all | solution.py:269
  70.0 0.6 add_shares.1
  (1 shorter events, 0.0 us)
Async XLA Ops:
  0.6 0.7 copy-start.4
  1.3 0.7 copy-start.3
  22.3 9.4 %copy-start.1 = (s32[2,1024]{1,0:T(2,128)S(1)}, s32[2,1024]{1,0:T(2,128)}, u32[]{:S(2)}) copy-start(s32[2,1024]{1,0:T(2,128)} %cells.1) | copy-start | bytes 24580
  22.3 9.4 %copy-start.2 = (f32[2,1024]{1,0:T(2,128)S(1)}, f32[2,1024]{1,0:T(2,128)}, u32[]{:S(2)}) copy-start(f32[2,1024]{1,0:T(2,128)} %fractions.1) | copy-start | bytes 24580
  22.3 4.7 %collective-permute-start.2 = (bf16[256,128]{1,0:T(8,128)(2,1)S(1)}, bf16[256,128]{1,0:T(8,128)(2,1)S(1)}, u32[]{:S(2)}, u32[]{:S(2)}) collective-permute-start(bf16[256,128]{1,0:T(8,128)(2,1)S(1)} %bitcast.5), channel_id=1, source_target_pairs={{0,192},{64,0},{128,64},{192,128},{1,193},{65,1},{129,65},{193,129... | collective-permute-start | bytes 196616 | tf_op jit(solution)/shard_map/ppermute | solution.py:227
  25.1 5.8 %collective-permute-start.1 = (bf16[256,128]{1,0:T(8,128)(2,1)S(1)}, bf16[256,128]{1,0:T(8,128)(2,1)S(1)}, u32[]{:S(2)}, u32[]{:S(2)}) collective-permute-start(bf16[256,128]{1,0:T(8,128)(2,1)S(1)} %bitcast.6), channel_id=1, source_target_pairs={{0,128},{64,192},{128,0},{192,64},{1,129},{65,193},{129,1},{193,65... | collective-permute-start | bytes 196616 | tf_op jit(solution)/shard_map/ppermute | solution.py:227
  25.9 5.7 %collective-permute-start = (bf16[256,128]{1,0:T(8,128)(2,1)S(1)}, bf16[256,128]{1,0:T(8,128)(2,1)S(1)}, u32[]{:S(2)}, u32[]{:S(2)}) collective-permute-start(bf16[256,128]{1,0:T(8,128)(2,1)S(1)} %bitcast.7), channel_id=1, source_target_pairs={{0,64},{64,128},{128,192},{192,0},{1,65},{65,129},{129,193},{193,1... | collective-permute-start | bytes 196616 | tf_op jit(solution)/shard_map/ppermute | solution.py:227
  31.6 3.6 %copy-start = (bf16[1024,128]{1,0:T(8,128)(2,1)S(1)}, bf16[1024,128]{1,0:T(8,128)(2,1)}, u32[]{:S(2)}) copy-start(bf16[1024,128]{1,0:T(8,128)(2,1)} %observed.1) | copy-start | bytes 786436
  31.6 3.5 %collective-permute-start.3 = (bf16[1024,128]{1,0:T(8,128)(2,1)S(1)}, bf16[1024,128]{1,0:T(8,128)(2,1)S(1)}, u32[]{:S(2)}, u32[]{:S(2)}) collective-permute-start(bf16[1024,128]{1,0:T(8,128)(2,1)S(1)} %pad_maximum_fusion), channel_id=1, source_target_pairs={{0,1},{1,0},{2,3},{3,2},{4,5},{5,4},{6,7},{7,6},{8,9},{9,8},{10,11... | collective-permute-start | bytes 786440 | tf_op jit(solution)/shard_map/ppermute | solution.py:230
  35.1 0.7 copy-start.5
  35.1 0.7 copy-start.6

commit v6 on v5

--- a/solution.py
+++ b/solution.py
@@ -31,7 +31,8 @@
     return [first, second, rest - second]
 
 
-def component_kernel(spectra, positions, out):
+def component_kernel(spectra, positions, counts, out, near_counts):
+    near_counts[...] = counts[...]
     count, channels = spectra.shape
     pixels = positions[...]
     low = ((pixels + 64) & 127) - 64
@@ -93,7 +94,14 @@
 
 
 def first_kernel(*refs):
-    pieces, (cells, fractions, factors, cos_out, sin_out) = refs[:-5], refs[-5:]
+    pieces, rest = refs[:-7], refs[-7:]
+    cells, fractions, weights, factors, cos_out, sin_out, weight_rows = rest
+    w = weights[...]
+    both = jnp.concatenate([w, w], axis=1)
+    lane = lax.broadcasted_iota(jnp.int32, both.shape, 1)
+    w_re = three_parts(jnp.where(lane < 64, both, 0.0))
+    w_im = three_parts(jnp.where(lane < 64, 0.0, both))
+    weight_rows[...] = jnp.concatenate(w_re + w_im + [jnp.zeros((2, 128), F32)]).astype(BF16)
     rows = factors.shape[0]
     parts = row_factors(cells[...], fractions[...])
     lead = jnp.zeros((DIGIT_LANE, rows), F32)
@@ -108,9 +116,9 @@
     sin_out[...] = sin_sum
 
 
-def second_kernel(
-    counts, comps, factors, cos_in, sin_in, cells, fractions, observed, weights, residual, packed, fields
-):
+def second_kernel(counts, *refs):
+    pieces, rest = refs[:-10], refs[-10:]
+    factors, cos_in, sin_in, cells, fractions, observed, weights, residual, packed, fields = rest
     rows = observed.shape[0]
     owners, tiles, _, slot = packed.shape
     start = []
@@ -119,14 +127,9 @@
         start.append(total)
         total = total + counts[0, t]
 
-    w = weights[...]
-    both = jnp.concatenate([w, w], axis=1)
-    lane = lax.broadcasted_iota(jnp.int32, both.shape, 1)
-    w_re = three_parts(jnp.where(lane < 64, both, 0.0))
-    w_im = three_parts(jnp.where(lane < 64, 0.0, both))
-    w_rows = jnp.concatenate(w_re + w_im + [jnp.zeros((2, 128), F32)]).astype(BF16)
-
-    cos_sum, sin_sum = add_products(factors[...], comps, cos_in[...], sin_in[...])
+    cos_sum, sin_sum = cos_in[...], sin_in[...]
+    for comps in pieces:
+        cos_sum, sin_sum = add_products(factors[...], comps, cos_sum, sin_sum)
     lanes = lax.broadcasted_iota(jnp.int32, (rows, 128), 1)
     index = lax.broadcasted_iota(jnp.int32, (rows, 128), 0)
     real = cos_sum * SIN_POLY[-1] ** 2
@@ -134,7 +137,7 @@
     predicted = jnp.where(lanes < 64, real, imag)
     res = jnp.where(index < total, observed[...].astype(F32) - predicted, 0.0).astype(BF16)
     residual[...] = res
-    sums = lax.dot_general(w_rows, res, NT, preferred_element_type=F32)
+    sums = lax.dot_general(weights[...], res, NT, preferred_element_type=F32)
     fields[0:1, :] = sums[0:1] + sums[1:2] + sums[2:3]
     fields[1:2, :] = sums[3:4] + sums[4:5] + sums[5:6]
     fields[2:4, :] = cells[...].astype(F32) + 0.5 * fractions[...]
@@ -160,7 +163,9 @@
     return jnp.exp2(off * off * -0.7213475204444817), (first + tap) >> 3
 
 
-def grid_kernel(got, out, acc):
+def grid_kernel(got, near, out, far, acc, sem):
+    leave = pltpu.make_async_copy(near, far, sem)
+    leave.start()
     sources, _, slot = got.shape
     group = 16
     count = group * slot
@@ -191,6 +196,7 @@
         imag = acc[BAND + 8 * g : BAND + 8 * g + 8]
         out[2 * g] = jnp.where(upper, real, pltpu.roll(imag, 4, 0)).astype(BF16)
         out[2 * g + 1] = jnp.where(upper, pltpu.roll(real, 4, 0), imag).astype(BF16)
+    leave.wait()
 
 
 def sum_kernel(got, out):
@@ -209,63 +215,72 @@
     owners = lax.axis_size(VIS)
     slot = rows // 2
     width = GRID // tiles
-    plane = ("vis_1", "tile_0")
+    plane = VIS + ("tile_0",)
     members = lax.axis_size(plane)
     count = spectra.shape[1]
+    line = lax.axis_size("vis_0")
     vmem = pl.BlockSpec(memory_space=pltpu.VMEM)
-    mine = pl.pallas_call(
+    far = pl.BlockSpec(memory_space=pltpu.HBM)
+    mine, near_counts = pl.pallas_call(
         component_kernel,
-        out_shape=jax.ShapeDtypeStruct((members, count, 128), BF16),
-        in_specs=[vmem] * 2,
-        out_specs=vmem,
+        out_shape=(
+            jax.ShapeDtypeStruct((members, count, 128), BF16),
+            jax.ShapeDtypeStruct(bucket_counts.shape, jnp.int32),
+        ),
+        in_specs=[vmem] * 3,
+        out_specs=(vmem,) * 2,
         name="components",
         compiler_params=LIMIT,
-    )(spectra.T, positions)
+    )(spectra.T, positions, bucket_counts)
     own = lax.all_to_all(mine, plane, 0, 0, tiled=True).reshape(members * count, 128)
-    line = lax.axis_size("vis_0")
-    here = [own] + [
-        lax.ppermute(own, "vis_0", [(k, (k + step) % line) for k in range(line)])
-        for step in range(1, line)
-    ]
-    there = lax.ppermute(jnp.concatenate(here), "tile_1", [(0, 1), (1, 0)])
+    here = [own]
+    there = [lax.ppermute(own, "tile_1", [(0, 1), (1, 0)])]
     sums = jax.ShapeDtypeStruct((rows, 128), F32)
-    factors, cos_sum, sin_sum = pl.pallas_call(
+    factors, cos_sum, sin_sum, weight_rows = pl.pallas_call(
         first_kernel,
-        out_shape=(jax.ShapeDtypeStruct((rows, 128), BF16), sums, sums),
-        in_specs=[vmem] * (line + 2),
-        out_specs=(vmem,) * 3,
+        out_shape=(
+            jax.ShapeDtypeStruct((rows, 128), BF16),
+            sums,
+            sums,
+            jax.ShapeDtypeStruct((8, 128), BF16),
+        ),
+        in_specs=[vmem] * (len(here) + 3),
+        out_specs=(vmem,) * 4,
         name="predict_first",
         compiler_params=LIMIT,
-    )(*here, cells, fractions)
-    residual, packed = pl.pallas_call(
+    )(*here, cells, fractions, chan_weights[None, :])
+    near_residual, packed = pl.pallas_call(
         second_kernel,
         out_shape=(
             jax.ShapeDtypeStruct(observed.shape, BF16),
             jax.ShapeDtypeStruct((line, tiles, 4, slot), F32),
         ),
-        in_specs=[pl.BlockSpec(memory_space=pltpu.SMEM)] + [vmem] * 8,
+        in_specs=[pl.BlockSpec(memory_space=pltpu.SMEM)] + [vmem] * (7 + len(there)),
         out_specs=(vmem, vmem),
         scratch_shapes=[pltpu.VMEM((8, rows), F32)],
         name="predict_second",
         compiler_params=LIMIT,
     )(
-        bucket_counts, there, factors, cos_sum, sin_sum,
-        cells, fractions, observed, chan_weights[None, :],
+        near_counts, *there, factors, cos_sum, sin_sum,
+        cells, fractions, observed, weight_rows,
     )
     got = lax.all_to_all(
         packed.reshape(line * tiles, 4, slot), ("vis_0",) + TILE, 0, 0, tiled=True
     )
     share = BAND // owners
     block = width // line
-    partial = pl.pallas_call(
+    partial, residual = pl.pallas_call(
         grid_kernel,
-        out_shape=jax.ShapeDtypeStruct((owners, 2 * share, block), BF16),
-        in_specs=[vmem],
-        out_specs=vmem,
-        scratch_shapes=[pltpu.VMEM((2 * BAND, block), F32)],
+        out_shape=(
+            jax.ShapeDtypeStruct((owners, 2 * share, block), BF16),
+            jax.ShapeDtypeStruct(observed.shape, BF16),
+        ),
+        in_specs=[vmem] * 2,
+        out_specs=(vmem, far),
+        scratch_shapes=[pltpu.VMEM((2 * BAND, block), F32), pltpu.SemaphoreType.DMA],
         name="gridding",
         compiler_params=LIMIT,
-    )(got)
+    )(got, near_residual)
     parts = lax.all_to_all(partial, VIS, 0, 0, tiled=True)
     total = pl.pallas_call(
         sum_kernel,

time: 71 us -> 69.9 us (0.985)
  blocking collectives: 47.2 us -> 56.4 us
  waiting for transfers between devices: 4.79 us -> 0.01 us
  starting transfers between devices: 4.54 us -> 0.01 us
    all_to_all x1, blocking collectives: 20.2 us -> 29.2 us  [on_device(): lax.all_to_all(mine, plane, 0, 0, tiled=True).reshape(members * count, 128)]
    ppermute x4 -> x1, waiting for transfers between devices: 4.79 us -> 0.01 us  [on_device(): there = [lax.ppermute(own, 'tile_1', [(0, 1), (1, 0)])]]
    ppermute x4 -> x1, starting transfers between devices: 4.54 us -> 0.01 us  [on_device(): there = [lax.ppermute(own, 'tile_1', [(0, 1), (1, 0)])]]
  transfers between devices with their start and end apart: 4 -> 1, of which waited for: 3 -> 0; matrix products, arithmetic and copies ran while one was open for 0% -> 0% of each run, Pallas kernels for 5% -> 5%
where the time goes in v6:
time: 69.9 us; the launch traced here: 69.5 us
  blocking collectives  56.4 us (81%)
  Pallas kernels  11 us (16%)
  local copies, waits for them, and re-layouts  1.38 us (2%)
  between operations  0.73 us (1%)
    all_to_all x1, blocking collectives, on_device(): lax.all_to_all(mine, plane, 0, 0, tiled=True).reshape(members * count, 128)  29.2 us
    all_to_all x1, blocking collectives, on_device(): parts = lax.all_to_all(partial, VIS, 0, 0, tiled=True)  14.3 us
    all_to_all x1, blocking collectives, on_device(): lax.all_to_all(packed.reshape(line * tiles, 4, slot), ('vis_0',) + TILE,...  13 us
    pallas_call x1, Pallas kernels, on_device(): pl.pallas_call(second_kernel, out_shape=(jax.ShapeDtypeStruct(observed.sh...  4.12 us
    pallas_call x1, Pallas kernels, on_device(): pl.pallas_call(first_kernel, out_shape=(jax.ShapeDtypeStruct((rows, 128),...  3.39 us
    pallas_call x1, Pallas kernels, on_device(): pl.pallas_call(grid_kernel, out_shape=(jax.ShapeDtypeStruct((owners, 2 *...  2.66 us
  transfers between devices with their start and end apart: 1, of which 0 were waited for; matrix products, arithmetic and copies ran while one was open for 0% of the time, Pallas kernels for 5%

profile of v6, /device:TPU:32, one launch (start us, length us, event | category | flops | bytes accessed | tf_op | source)
XLA Modules:
  0.0 69.5 jit_solution(3839072146639395750)
XLA Ops:
  0.6 0.0 copy-start.6
  0.6 0.0 copy-start.4
  0.6 0.6 copy-done.6
  1.3 0.0 copy-done.4
  1.3 0.0 copy-start.3
  1.3 0.7 copy-done.3
  2.0 0.2 components.1
  2.2 0.0 copy-start.1
  2.2 0.0 copy-start.2
  2.2 0.0 copy-start.5
  2.2 29.2 %all_to_all.15 = bf16[128,8,128]{2,1,0:T(8,128)(2,1)S(1)} all-to-all(bf16[128,8,128]{2,1,0:T(8,128)(2,1)S(1)} %get-tuple-element.13), channel_id=1, replica_groups=mesh['vis_0'=4,'vis_1'=8,'tile_0'=4,'tile_1'=2] {'vis_0','vis_1','tile_0'}, dimensions={0} | all-to-all | bytes 524288 | tf_op jit(solution)/shard_map/all_to_all | solution.py:235
  31.4 0.0 copy-start
  31.4 0.0 collective-permute-start
  31.4 0.0 copy-done.1
  31.4 0.0 copy-done.2
  31.4 0.0 copy-done.5
  31.4 3.4 %predict_first.1 = (bf16[1024,128]{1,0:T(8,128)(2,1)S(1)}, f32[1024,128]{1,0:T(8,128)S(1)}, f32[1024,128]{1,0:T(8,128)S(1)}, bf16[8,128]{1,0:T(8,128)(2,1)S(1)}) custom-call(bf16[1024,128]{1,0:T(8,128)(2,1)S(1)} %bitcast.6, s32[2,1024]{1,0:T(2,128)S(1)} %copy-done.1, f32[2,1024]{1,0:T(2,128)S(1)} %copy-done.2, f32[1,64]{1,0:T(1,128)S(1)} %bitcast.10), custom_call_target="tpu_custom_call" | custom-call | tf_op jit(solution)/shard_map/predict_first/pallas_call | solution.py:239
  34.8 0.0 collective-permute-done.refs_0_
  34.8 0.0 copy-done
  34.8 4.1 %predict_second.1 = (bf16[1024,128]{1,0:T(8,128)(2,1)S(1)}, f32[4,8,4,512]{3,2,1,0:T(4,128)S(1)}) custom-call(s32[1,8]{1,0:T(1,128)S(1)} %get-tuple-element.12.counts, bf16[1024,128]{1,0:T(8,128)(2,1)S(1)} %collective-permute-done.refs_0_, bf16[1024,128]{1,0:T(8,128)(2,1)S(1)} %get-tuple-element.14.refs_1_, f32[1024,128]{1,0:T(8,128)S(1)} %get-tuple-element.15.refs_2_, ...), custom_call_target="tpu_custom_call" | custom-call | tf_op jit(solution)/shard_map/predict_second/pallas_call | solution.py:252
  38.9 13.0 %all_to_all.16.got = f32[32,4,512]{2,1,0:T(4,128)S(1)} all-to-all(f32[32,4,512]{2,1,0:T(4,128)S(1)} %bitcast.8), channel_id=1, replica_groups=mesh['vis_0'=4,'vis_1'=8,'tile_0'=4,'tile_1'=2] {'vis_0','tile_0','tile_1'}, dimensions={0} | all-to-all | bytes 524288 | tf_op jit(solution)/shard_map/all_to_all | solution.py:267
  51.9 2.7 %gridding.1 = (bf16[32,8,256]{2,1,0:T(8,128)(2,1)S(1)}, bf16[1024,128]{1,0:T(8,128)(2,1)}) custom-call(f32[32,4,512]{2,1,0:T(4,128)S(1)} %all_to_all.16.got, bf16[1024,128]{1,0:T(8,128)(2,1)S(1)} %get-tuple-element.19.near), custom_call_target="tpu_custom_call" | custom-call | tf_op jit(solution)/shard_map/gridding/pallas_call | solution.py:272
  54.6 14.3 %all_to_all.17 = bf16[32,8,256]{2,1,0:T(8,128)(2,1)S(1)} all-to-all(bf16[32,8,256]{2,1,0:T(8,128)(2,1)S(1)} %get-tuple-element.21), channel_id=1, replica_groups=mesh['vis_0'=4,'vis_1'=8,'tile_0'=4,'tile_1'=2] {'vis_0','vis_1'}, dimensions={0} | all-to-all | bytes 262144 | tf_op jit(solution)/shard_map/all_to_all | solution.py:284
  68.9 0.6 add_shares.1
Async XLA Ops:
  0.6 0.7 copy-start.6
  0.6 0.7 copy-start.4
  1.3 0.7 copy-start.3
  2.2 29.2 %copy-start.1 = (s32[2,1024]{1,0:T(2,128)S(1)}, s32[2,1024]{1,0:T(2,128)}, u32[]{:S(2)}) copy-start(s32[2,1024]{1,0:T(2,128)} %refs_4_.1) | copy-start | bytes 24580
  2.2 29.2 %copy-start.2 = (f32[2,1024]{1,0:T(2,128)S(1)}, f32[2,1024]{1,0:T(2,128)}, u32[]{:S(2)}) copy-start(f32[2,1024]{1,0:T(2,128)} %refs_5_.1) | copy-start | bytes 24580
  2.2 29.2 %copy-start.5 = (f32[64]{0:T(128)S(1)}, f32[64]{0:T(128)}, u32[]{:S(2)}) copy-start(f32[64]{0:T(128)} %param.13) | copy-start | bytes 772
  31.4 3.4 %copy-start = (bf16[1024,128]{1,0:T(8,128)(2,1)S(1)}, bf16[1024,128]{1,0:T(8,128)(2,1)}, u32[]{:S(2)}) copy-start(bf16[1024,128]{1,0:T(8,128)(2,1)} %refs_6_.1) | copy-start | bytes 786436
  31.4 3.4 %collective-permute-start = (bf16[1024,128]{1,0:T(8,128)(2,1)S(1)}, bf16[1024,128]{1,0:T(8,128)(2,1)S(1)}, u32[]{:S(2)}, u32[]{:S(2)}) collective-permute-start(bf16[1024,128]{1,0:T(8,128)(2,1)S(1)} %bitcast.5), channel_id=1, source_target_pairs={{0,1},{1,0},{2,3},{3,2},{4,5},{5,4},{6,7},{7,6},{8,9},{9,8},{10,11... | collective-permute-start | bytes 786440 | tf_op jit(solution)/shard_map/ppermute | solution.py:237

commit v7 on v6

--- a/solution.py
+++ b/solution.py
@@ -10,8 +10,9 @@
 BAND = 128
 TAPS = 8
 TILE = ("tile_0", "tile_1")
-VIS = ("vis_0", "vis_1")
-VIS_TILE = ("vis_0", "vis_1", "tile_0", "tile_1")
+LINE = ("vis_a", "vis_b")
+VIS = ("vis_a", "vis_b", "vis_1")
+VIS_TILE = ("vis_a", "vis_b", "vis_1", "tile_0", "tile_1")
 DIGIT_LANE = 64
 F32 = jnp.float32
 BF16 = jnp.bfloat16
@@ -78,7 +79,7 @@
 
 
 def add_products(left, comps, cos_sum, sin_sum):
-    comp_block = 256
+    comp_block = 512
     for first in range(0, comps.shape[0], comp_block):
         piece = comps[first : first + comp_block, :]
         turns = lax.dot_general(left, piece, NT, preferred_element_type=F32)
@@ -112,6 +113,15 @@
     sin_sum = jnp.zeros((rows, 128), F32)
     for comps in pieces:
         cos_sum, sin_sum = add_products(left, comps, cos_sum, sin_sum)
+    cos_out[...] = cos_sum
+    sin_out[...] = sin_sum
+
+
+def middle_kernel(*refs):
+    pieces, (factors, cos_in, sin_in, cos_out, sin_out) = refs[:-5], refs[-5:]
+    cos_sum, sin_sum = cos_in[...], sin_in[...]
+    for comps in pieces:
+        cos_sum, sin_sum = add_products(factors[...], comps, cos_sum, sin_sum)
     cos_out[...] = cos_sum
     sin_out[...] = sin_sum
 
@@ -215,10 +225,10 @@
     owners = lax.axis_size(VIS)
     slot = rows // 2
     width = GRID // tiles
-    plane = VIS + ("tile_0",)
+    plane = ("vis_a", "vis_1", "tile_0")
     members = lax.axis_size(plane)
     count = spectra.shape[1]
-    line = lax.axis_size("vis_0")
+    line = lax.axis_size(LINE)
     vmem = pl.BlockSpec(memory_space=pltpu.VMEM)
     far = pl.BlockSpec(memory_space=pltpu.HBM)
     mine, near_counts = pl.pallas_call(
@@ -233,8 +243,10 @@
         compiler_params=LIMIT,
     )(spectra.T, positions, bucket_counts)
     own = lax.all_to_all(mine, plane, 0, 0, tiled=True).reshape(members * count, 128)
+    swap = [(0, 1), (1, 0)]
     here = [own]
-    there = [lax.ppermute(own, "tile_1", [(0, 1), (1, 0)])]
+    next_to = lax.ppermute(own, "vis_b", swap)
+    other = lax.ppermute(own, "tile_1", swap)
     sums = jax.ShapeDtypeStruct((rows, 128), F32)
     factors, cos_sum, sin_sum, weight_rows = pl.pallas_call(
         first_kernel,
@@ -249,13 +261,25 @@
         name="predict_first",
         compiler_params=LIMIT,
     )(*here, cells, fractions, chan_weights[None, :])
+    middle = pl.pallas_call(
+        middle_kernel,
+        out_shape=(sums, sums),
+        in_specs=[vmem] * 4,
+        out_specs=(vmem, vmem),
+        name="predict_middle",
+        compiler_params=LIMIT,
+    )
+    cos_sum, sin_sum = middle(other, factors, cos_sum, sin_sum)
+    next_to, cos_sum, sin_sum = lax.optimization_barrier((next_to, cos_sum, sin_sum))
+    there = [lax.ppermute(next_to, "tile_1", swap)]
+    cos_sum, sin_sum = middle(next_to, factors, cos_sum, sin_sum)
     near_residual, packed = pl.pallas_call(
         second_kernel,
         out_shape=(
             jax.ShapeDtypeStruct(observed.shape, BF16),
             jax.ShapeDtypeStruct((line, tiles, 4, slot), F32),
         ),
-        in_specs=[pl.BlockSpec(memory_space=pltpu.SMEM)] + [vmem] * (7 + len(there)),
+        in_specs=[pl.BlockSpec(memory_space=pltpu.SMEM)] + [vmem] * 8,
         out_specs=(vmem, vmem),
         scratch_shapes=[pltpu.VMEM((8, rows), F32)],
         name="predict_second",
@@ -265,7 +289,7 @@
         cells, fractions, observed, weight_rows,
     )
     got = lax.all_to_all(
-        packed.reshape(line * tiles, 4, slot), ("vis_0",) + TILE, 0, 0, tiled=True
+        packed.reshape(line * tiles, 4, slot), LINE + TILE, 0, 0, tiled=True
     )
     share = BAND // owners
     block = width // line
@@ -294,7 +318,7 @@
 
 
 def solution(mesh):
-    torus = Mesh(mesh.devices.reshape(4, 8, 4, 2), ("vis_0", "vis_1", "tile_0", "tile_1"))
+    torus = Mesh(mesh.devices.reshape(2, 2, 8, 4, 2), VIS_TILE)
     return jax.shard_map(
         on_device,
         mesh=torus,

time: 69.9 us -> 68.6 us (0.981)
  blocking collectives: 56.4 us -> 52.5 us
  waiting for transfers between devices: 0.01 us -> 1.81 us
    pallas_call x0 -> x2, Pallas kernels: none -> 3.4 us  [the longest x1 1.71 us: on_device(): cos_sum, sin_sum = middle(other, factors, cos_sum, sin_sum)]
    all_to_all x1, blocking collectives: 29.2 us -> 26.1 us  [on_device(): lax.all_to_all(mine, plane, 0, 0, tiled=True).reshape(members * count, 128)]
    ppermute x1 -> x3, waiting for transfers between devices: 0.01 us -> 1.81 us  [the longest x1 1.8 us: on_device(): next_to = lax.ppermute(own, 'vis_b', swap)]
    pallas_call x1, Pallas kernels: 3.39 us -> 1.72 us  [on_device(): pl.pallas_call(first_kernel, out_shape=(jax.ShapeDtypeStruct((rows, 128),...]
    pallas_call x1, Pallas kernels: 4.12 us -> 2.63 us  [on_device(): pl.pallas_call(second_kernel, out_shape=(jax.ShapeDtypeStruct(observed.sh...]
    all_to_all x1, blocking collectives: 13 us -> 11.9 us  [on_device(): lax.all_to_all(packed.reshape(line * tiles, 4, slot), LINE + TILE, 0, 0,...]
  transfers between devices with their start and end apart: 1 -> 3, of which waited for: 0 -> 1; matrix products, arithmetic and copies ran while one was open for 0% -> 0% of each run, Pallas kernels for 5% -> 8%
where the time goes in v7:
time: 68.6 us; the launch traced here: 68.3 us
  blocking collectives  52.5 us (77%)
  Pallas kernels  11.2 us (16%)
  waiting for transfers between devices  1.81 us (3%)
  local copies, waits for them, and re-layouts  1.43 us (2%)
  between operations  0.74 us (1%)
    all_to_all x1, blocking collectives, on_device(): lax.all_to_all(mine, plane, 0, 0, tiled=True).reshape(members * count, 128)  26.1 us
    all_to_all x1, blocking collectives, on_device(): parts = lax.all_to_all(partial, VIS, 0, 0, tiled=True)  14.5 us
    all_to_all x1, blocking collectives, on_device(): lax.all_to_all(packed.reshape(line * tiles, 4, slot), LINE + TILE, 0, 0,...  11.9 us
    pallas_call x1, Pallas kernels, on_device(): pl.pallas_call(grid_kernel, out_shape=(jax.ShapeDtypeStruct((owners, 2 *...  2.66 us
    pallas_call x1, Pallas kernels, on_device(): pl.pallas_call(second_kernel, out_shape=(jax.ShapeDtypeStruct(observed.sh...  2.63 us
    ppermute x1, waiting for transfers between devices, on_device(): next_to = lax.ppermute(own, 'vis_b', swap)  1.8 us
    pallas_call x1, Pallas kernels, on_device(): pl.pallas_call(first_kernel, out_shape=(jax.ShapeDtypeStruct((rows, 128),...  1.72 us
    pallas_call x1, Pallas kernels, on_device(): cos_sum, sin_sum = middle(other, factors, cos_sum, sin_sum)  1.71 us
  transfers between devices with their start and end apart: 3, of which 1 were waited for; matrix products, arithmetic and copies ran while one was open for 0% of the time, Pallas kernels for 8%

profile of v7, /device:TPU:32, one launch (start us, length us, event | category | flops | bytes accessed | tf_op | source)
XLA Modules:
  0.0 68.3 jit_solution(20032614661250304)
XLA Ops:
  0.6 0.0 copy-start.6
  0.6 0.0 copy-start.4
  0.6 0.6 copy-done.6
  1.3 0.0 copy-done.4
  1.3 0.0 copy-start.3
  1.3 0.7 copy-done.3
  2.0 0.2 components.1
  2.2 0.0 copy-start.1
  2.2 0.0 copy-start.2
  2.2 26.1 %all_to_all.15 = bf16[64,8,128]{2,1,0:T(8,128)(2,1)S(1)} all-to-all(bf16[64,8,128]{2,1,0:T(8,128)(2,1)S(1)} %get-tuple-element.20), channel_id=1, replica_groups=mesh['vis_a'=2,'vis_b'=2,'vis_1'=8,'tile_0'=4,'tile_1'=2] {'vis_a','vis_..., dimensions={0} | all-to-all | bytes 262144 | tf_op jit(solution)/shard_map/all_to_all | solution.py:245
  28.3 0.0 copy-start.5
  28.3 0.0 collective-permute-start.1
  28.3 0.6 collective-permute-start
  28.9 0.0 copy-done.1
  28.9 0.0 copy-done.2
  28.9 0.1 copy-done.5
  28.9 1.7 %predict_first.1 = (bf16[1024,128]{1,0:T(8,128)(2,1)S(1)}, f32[1024,128]{1,0:T(8,128)S(1)}, f32[1024,128]{1,0:T(8,128)S(1)}, bf16[8,128]{1,0:T(8,128)(2,1)S(1)}) custom-call(bf16[512,128]{1,0:T(8,128)(2,1)S(1)} %bitcast.8, s32[2,1024]{1,0:T(2,128)S(1)} %copy-done.1, f32[2,1024]{1,0:T(2,128)S(1)} %copy-done.2, f32[1,64]{1,0:T(1,128)S(1)} %bitcast.11), custom_call_target="tpu_custom_call" | custom-call | tf_op jit(solution)/shard_map/predict_first/pallas_call | solution.py:251
  30.7 0.0 collective-permute-done.1.refs_0_
  30.7 1.7 %predict_middle.2 = (f32[1024,128]{1,0:T(8,128)S(1)}, f32[1024,128]{1,0:T(8,128)S(1)}) custom-call(bf16[512,128]{1,0:T(8,128)(2,1)S(1)} %collective-permute-done.1.refs_0_, bf16[1024,128]{1,0:T(8,128)(2,1)S(1)} %get-tuple-element.21.refs_1_, f32[1024,128]{1,0:T(8,128)S(1)} %get-tuple-element.22.refs_2_, f32[1024,128]{1,0:T(8,128)S(1)} %get-tuple-element.23.refs_3_), custom_call_target="tpu_custom_call" | custom-call | tf_op jit(solution)/shard_map/predict_middle/pallas_call | solution.py:272
  32.4 1.8 %collective-permute-done.refs_0_ = bf16[512,128]{1,0:T(8,128)(2,1)S(1)} collective-permute-done((bf16[512,128]{1,0:T(8,128)(2,1)S(1)}, bf16[512,128]{1,0:T(8,128)(2,1)S(1)}, u32[]{:S(2)}, u32[]{:S(2)}) %collective-permute-start) | collective-permute-done | bytes 131104 | tf_op jit(solution)/shard_map/ppermute | solution.py:248
  34.2 0.0 copy-start
  34.2 0.0 collective-permute-start.2
  34.2 1.7 %predict_middle.3 = (f32[1024,128]{1,0:T(8,128)S(1)}, f32[1024,128]{1,0:T(8,128)S(1)}) custom-call(bf16[512,128]{1,0:T(8,128)(2,1)S(1)} %collective-permute-done.refs_0_, bf16[1024,128]{1,0:T(8,128)(2,1)S(1)} %get-tuple-element.21.refs_1_, f32[1024,128]{1,0:T(8,128)S(1)} %get-tuple-element.27.refs_2_, f32[1024,128]{1,0:T(8,128)S(1)} %get-tuple-element.28.refs_3_), custom_call_target="tpu_custom_call" | custom-call | tf_op jit(solution)/shard_map/predict_middle/pallas_call | solution.py:275
  35.9 0.0 collective-permute-done.2.refs_0_
  35.9 0.0 copy-done
  35.9 2.6 %predict_second.1 = (bf16[1024,128]{1,0:T(8,128)(2,1)S(1)}, f32[4,8,4,512]{3,2,1,0:T(4,128)S(1)}) custom-call(s32[1,8]{1,0:T(1,128)S(1)} %get-tuple-element.19.counts, bf16[512,128]{1,0:T(8,128)(2,1)S(1)} %collective-permute-done.2.refs_0_, bf16[1024,128]{1,0:T(8,128)(2,1)S(1)} %get-tuple-element.21.refs_1_, f32[1024,128]{1,0:T(8,128)S(1)} %get-tuple-element.29.refs_2_, ...), custom_call_target="tpu_custom_call" | custom-call | tf_op jit(solution)/shard_map/predict_second/pallas_call | solution.py:276
  38.5 11.9 %all_to_all.16.got = f32[32,4,512]{2,1,0:T(4,128)S(1)} all-to-all(f32[32,4,512]{2,1,0:T(4,128)S(1)} %bitcast.9), channel_id=1, replica_groups=mesh['vis_a'=2,'vis_b'=2,'vis_1'=8,'tile_0'=4,'tile_1'=2] {'vis_a','vis_..., dimensions={0} | all-to-all | bytes 524288 | tf_op jit(solution)/shard_map/all_to_all | solution.py:291
  50.4 2.7 %gridding.1 = (bf16[32,8,256]{2,1,0:T(8,128)(2,1)S(1)}, bf16[1024,128]{1,0:T(8,128)(2,1)}) custom-call(f32[32,4,512]{2,1,0:T(4,128)S(1)} %all_to_all.16.got, bf16[1024,128]{1,0:T(8,128)(2,1)S(1)} %get-tuple-element.33.near), custom_call_target="tpu_custom_call" | custom-call | tf_op jit(solution)/shard_map/gridding/pallas_call | solution.py:296
  53.1 14.5 %all_to_all.17 = bf16[32,8,256]{2,1,0:T(8,128)(2,1)S(1)} all-to-all(bf16[32,8,256]{2,1,0:T(8,128)(2,1)S(1)} %get-tuple-element.35), channel_id=1, replica_groups=mesh['vis_a'=2,'vis_b'=2,'vis_1'=8,'tile_0'=4,'tile_1'=2] {'vis_a','vis_..., dimensions={0} | all-to-all | bytes 262144 | tf_op jit(solution)/shard_map/all_to_all | solution.py:308
  67.6 0.6 add_shares.1
Async XLA Ops:
  0.6 0.7 copy-start.6
  0.6 0.7 %copy-start.4 = (s32[2,8]{1,0:T(2,128)S(1)}, s32[2,8]{1,0:T(2,128)}, u32[]{:S(2)}) copy-start(s32[2,8]{1,0:T(2,128)} %positions.1) | copy-start | bytes 196
  1.3 0.7 copy-start.3
  2.2 26.7 %copy-start.1 = (s32[2,1024]{1,0:T(2,128)S(1)}, s32[2,1024]{1,0:T(2,128)}, u32[]{:S(2)}) copy-start(s32[2,1024]{1,0:T(2,128)} %refs_4_.1) | copy-start | bytes 24580
  2.2 26.7 %copy-start.2 = (f32[2,1024]{1,0:T(2,128)S(1)}, f32[2,1024]{1,0:T(2,128)}, u32[]{:S(2)}) copy-start(f32[2,1024]{1,0:T(2,128)} %refs_5_.1) | copy-start | bytes 24580
  28.3 0.7 copy-start.5
  28.3 2.4 %collective-permute-start.1 = (bf16[512,128]{1,0:T(8,128)(2,1)S(1)}, bf16[512,128]{1,0:T(8,128)(2,1)S(1)}, u32[]{:S(2)}, u32[]{:S(2)}) collective-permute-start(bf16[512,128]{1,0:T(8,128)(2,1)S(1)} %bitcast.6), channel_id=1, source_target_pairs={{0,1},{1,0},{2,3},{3,2},{4,5},{5,4},{6,7},{7,6},{8,9},{9,8},{10,11... | collective-permute-start | bytes 393224 | tf_op jit(solution)/shard_map/ppermute | solution.py:249
  28.3 5.9 %collective-permute-start = (bf16[512,128]{1,0:T(8,128)(2,1)S(1)}, bf16[512,128]{1,0:T(8,128)(2,1)S(1)}, u32[]{:S(2)}, u32[]{:S(2)}) collective-permute-start(bf16[512,128]{1,0:T(8,128)(2,1)S(1)} %bitcast.7), channel_id=1, source_target_pairs={{0,64},{64,0},{1,65},{65,1},{2,66},{66,2},{3,67},{67,3},{4,68},{68... | collective-permute-start | bytes 393224 | tf_op jit(solution)/shard_map/ppermute | solution.py:248
  34.2 1.7 %copy-start = (bf16[1024,128]{1,0:T(8,128)(2,1)S(1)}, bf16[1024,128]{1,0:T(8,128)(2,1)}, u32[]{:S(2)}) copy-start(bf16[1024,128]{1,0:T(8,128)(2,1)} %refs_6_.1) | copy-start | bytes 786436
  34.2 1.7 %collective-permute-start.2 = (bf16[512,128]{1,0:T(8,128)(2,1)S(1)}, bf16[512,128]{1,0:T(8,128)(2,1)S(1)}, u32[]{:S(2)}, u32[]{:S(2)}) collective-permute-start(bf16[512,128]{1,0:T(8,128)(2,1)S(1)} %collective-permute-done.refs_0_), channel_id=1, source_target_pairs={{0,1},{1,0},{2,3},{3,2},{4,5},{5,4},{6,7},{7,6},{8,9},{9,8},{10,11... | collective-permute-start | bytes 393224 | tf_op jit(solution)/shard_map/ppermute | solution.py:274

commit v8 on v7

--- a/solution.py
+++ b/solution.py
@@ -8,7 +8,6 @@
 
 GRID = 8192
 BAND = 128
-TAPS = 8
 TILE = ("tile_0", "tile_1")
 LINE = ("vis_a", "vis_b")
 VIS = ("vis_a", "vis_b", "vis_1")
@@ -22,7 +21,6 @@
 COS_POLY = (1.41420408, -6.97764191, 5.71523647, -1.72834251)
 SIN_POLY = (4.4428679, -7.30744333, 3.59478717, -0.78437159)
 LIMIT = pltpu.CompilerParams(vmem_limit_bytes=24 * 2**20)
-ROUND = 12582912.0
 
 
 def three_parts(value):
@@ -71,19 +69,12 @@
     return result
 
 
-def polynomial(coefficients, s):
-    result = coefficients[-1] * s + coefficients[-2]
-    for c in coefficients[-3::-1]:
-        result = result * s + c
-    return result
-
-
 def add_products(left, comps, cos_sum, sin_sum):
     comp_block = 512
     for first in range(0, comps.shape[0], comp_block):
         piece = comps[first : first + comp_block, :]
         turns = lax.dot_general(left, piece, NT, preferred_element_type=F32)
-        y = turns - ((turns + ROUND) - ROUND)
+        y = turns - jnp.round(turns)
         s = y * y
         c = monic(COS_POLY, s)
         d = monic(SIN_POLY, s) * y
@@ -177,7 +168,7 @@
     leave = pltpu.make_async_copy(near, far, sem)
     leave.start()
     sources, _, slot = got.shape
-    group = 16
+    group = 32
     count = group * slot
     width = out.shape[2]
     acc[...] = jnp.zeros(acc.shape, F32)
@@ -210,7 +201,7 @@
 
 
 def sum_kernel(got, out):
-    blocks, sources, lines, width = got.shape
+    blocks, _, lines, width = got.shape
     share = lines // 2
     for b in range(blocks):
         total = jnp.sum(got[b].astype(F32), axis=0)

time: 68.6 us -> 68.2 us (level)
  transfers between devices with their start and end apart: 3 -> 3, of which waited for: 1 -> 1; matrix products, arithmetic and copies ran while one was open for 0% -> 0% of each run, Pallas kernels for 8% -> 7%
where the time goes in v8:
time: 68.2 us; the launch traced here: 67.9 us
  blocking collectives  52.5 us (77%)
  Pallas kernels  10.7 us (16%)
  waiting for transfers between devices  1.96 us (3%)
  local copies, waits for them, and re-layouts  1.43 us (2%)
  between operations  0.74 us (1%)
    all_to_all x1, blocking collectives, on_device(): lax.all_to_all(mine, plane, 0, 0, tiled=True).reshape(members * count, 128)  26.1 us
    all_to_all x1, blocking collectives, on_device(): parts = lax.all_to_all(partial, VIS, 0, 0, tiled=True)  14.5 us
    all_to_all x1, blocking collectives, on_device(): lax.all_to_all(packed.reshape(line * tiles, 4, slot), LINE + TILE, 0, 0,...  11.9 us
    pallas_call x1, Pallas kernels, on_device(): pl.pallas_call(second_kernel, out_shape=(jax.ShapeDtypeStruct(observed.sh...  2.57 us
    pallas_call x1, Pallas kernels, on_device(): pl.pallas_call(grid_kernel, out_shape=(jax.ShapeDtypeStruct((owners, 2 *...  2.4 us
    ppermute x1, waiting for transfers between devices, on_device(): next_to = lax.ppermute(own, 'vis_b', swap)  1.95 us
    pallas_call x1, Pallas kernels, on_device(): cos_sum, sin_sum = middle(other, factors, cos_sum, sin_sum)  1.65 us
    pallas_call x1, Pallas kernels, on_device(): pl.pallas_call(first_kernel, out_shape=(jax.ShapeDtypeStruct((rows, 128),...  1.64 us
  transfers between devices with their start and end apart: 3, of which 1 were waited for; matrix products, arithmetic and copies ran while one was open for 0% of the time, Pallas kernels for 7%

profile of v8, /device:TPU:32, one launch (start us, length us, event | category | flops | bytes accessed | tf_op | source)
XLA Modules:
  0.0 67.9 jit_solution(5352974375792102355)
XLA Ops:
  0.6 0.0 copy-start.6
  0.6 0.0 copy-start.4
  0.6 0.6 copy-done.6
  1.3 0.0 copy-done.4
  1.3 0.0 copy-start.3
  1.3 0.7 %copy-done.3 = bf16[64,8]{0,1:T(8,128)(2,1)S(1)} copy-done((bf16[64,8]{0,1:T(8,128)(2,1)S(1)}, bf16[64,8]{0,1:T(8,128)(2,1)}, u32[]{:S(2)}) %copy-start.3) | copy-done | bytes 1048
  2.0 0.2 components.1
  2.2 0.0 copy-start.1
  2.2 0.0 copy-start.2
  2.2 26.1 %all_to_all.15 = bf16[64,8,128]{2,1,0:T(8,128)(2,1)S(1)} all-to-all(bf16[64,8,128]{2,1,0:T(8,128)(2,1)S(1)} %get-tuple-element.20), channel_id=1, replica_groups=mesh['vis_a'=2,'vis_b'=2,'vis_1'=8,'tile_0'=4,'tile_1'=2] {'vis_a','vis_..., dimensions={0} | all-to-all | bytes 262144 | tf_op jit(solution)/shard_map/all_to_all | solution.py:236
  28.3 0.0 copy-start.5
  28.3 0.0 collective-permute-start.1
  28.3 0.6 collective-permute-start
  28.9 0.0 copy-done.1
  28.9 0.0 copy-done.2
  28.9 0.1 copy-done.5
  28.9 1.6 %predict_first.1 = (bf16[1024,128]{1,0:T(8,128)(2,1)S(1)}, f32[1024,128]{1,0:T(8,128)S(1)}, f32[1024,128]{1,0:T(8,128)S(1)}, bf16[8,128]{1,0:T(8,128)(2,1)S(1)}) custom-call(bf16[512,128]{1,0:T(8,128)(2,1)S(1)} %bitcast.8, s32[2,1024]{1,0:T(2,128)S(1)} %copy-done.1, f32[2,1024]{1,0:T(2,128)S(1)} %copy-done.2, f32[1,64]{1,0:T(1,128)S(1)} %bitcast.11), custom_call_target="tpu_custom_call" | custom-call | tf_op jit(solution)/shard_map/predict_first/pallas_call | solution.py:242
  30.6 0.0 collective-permute-done.1.refs_0_
  30.6 1.6 %predict_middle.2 = (f32[1024,128]{1,0:T(8,128)S(1)}, f32[1024,128]{1,0:T(8,128)S(1)}) custom-call(bf16[512,128]{1,0:T(8,128)(2,1)S(1)} %collective-permute-done.1.refs_0_, bf16[1024,128]{1,0:T(8,128)(2,1)S(1)} %get-tuple-element.21.refs_1_, f32[1024,128]{1,0:T(8,128)S(1)} %get-tuple-element.22.refs_2_, f32[1024,128]{1,0:T(8,128)S(1)} %get-tuple-element.23.refs_3_), custom_call_target="tpu_custom_call" | custom-call | tf_op jit(solution)/shard_map/predict_middle/pallas_call | solution.py:263
  32.2 2.0 %collective-permute-done.refs_0_ = bf16[512,128]{1,0:T(8,128)(2,1)S(1)} collective-permute-done((bf16[512,128]{1,0:T(8,128)(2,1)S(1)}, bf16[512,128]{1,0:T(8,128)(2,1)S(1)}, u32[]{:S(2)}, u32[]{:S(2)}) %collective-permute-start) | collective-permute-done | bytes 131104 | tf_op jit(solution)/shard_map/ppermute | solution.py:239
  34.2 0.0 copy-start
  34.2 0.0 collective-permute-start.2
  34.2 1.6 %predict_middle.3 = (f32[1024,128]{1,0:T(8,128)S(1)}, f32[1024,128]{1,0:T(8,128)S(1)}) custom-call(bf16[512,128]{1,0:T(8,128)(2,1)S(1)} %collective-permute-done.refs_0_, bf16[1024,128]{1,0:T(8,128)(2,1)S(1)} %get-tuple-element.21.refs_1_, f32[1024,128]{1,0:T(8,128)S(1)} %get-tuple-element.27.refs_2_, f32[1024,128]{1,0:T(8,128)S(1)} %get-tuple-element.28.refs_3_), custom_call_target="tpu_custom_call" | custom-call | tf_op jit(solution)/shard_map/predict_middle/pallas_call | solution.py:266
  35.8 0.0 collective-permute-done.2.refs_0_
  35.8 0.0 copy-done
  35.9 2.6 %predict_second.1 = (bf16[1024,128]{1,0:T(8,128)(2,1)S(1)}, f32[4,8,4,512]{3,2,1,0:T(4,128)S(1)}) custom-call(s32[1,8]{1,0:T(1,128)S(1)} %get-tuple-element.19.counts, bf16[512,128]{1,0:T(8,128)(2,1)S(1)} %collective-permute-done.2.refs_0_, bf16[1024,128]{1,0:T(8,128)(2,1)S(1)} %get-tuple-element.21.refs_1_, f32[1024,128]{1,0:T(8,128)S(1)} %get-tuple-element.29.refs_2_, ...), custom_call_target="tpu_custom_call" | custom-call | tf_op jit(solution)/shard_map/predict_second/pallas_call | solution.py:267
  38.4 11.9 %all_to_all.16.got = f32[32,4,512]{2,1,0:T(4,128)S(1)} all-to-all(f32[32,4,512]{2,1,0:T(4,128)S(1)} %bitcast.9), channel_id=1, replica_groups=mesh['vis_a'=2,'vis_b'=2,'vis_1'=8,'tile_0'=4,'tile_1'=2] {'vis_a','vis_..., dimensions={0} | all-to-all | bytes 524288 | tf_op jit(solution)/shard_map/all_to_all | solution.py:282
  50.3 2.4 %gridding.1 = (bf16[32,8,256]{2,1,0:T(8,128)(2,1)S(1)}, bf16[1024,128]{1,0:T(8,128)(2,1)}) custom-call(f32[32,4,512]{2,1,0:T(4,128)S(1)} %all_to_all.16.got, bf16[1024,128]{1,0:T(8,128)(2,1)S(1)} %get-tuple-element.33.near), custom_call_target="tpu_custom_call" | custom-call | tf_op jit(solution)/shard_map/gridding/pallas_call | solution.py:287
  52.7 14.5 %all_to_all.17 = bf16[32,8,256]{2,1,0:T(8,128)(2,1)S(1)} all-to-all(bf16[32,8,256]{2,1,0:T(8,128)(2,1)S(1)} %get-tuple-element.35), channel_id=1, replica_groups=mesh['vis_a'=2,'vis_b'=2,'vis_1'=8,'tile_0'=4,'tile_1'=2] {'vis_a','vis_..., dimensions={0} | all-to-all | bytes 262144 | tf_op jit(solution)/shard_map/all_to_all | solution.py:299
  67.2 0.6 add_shares.1
Async XLA Ops:
  0.6 0.7 copy-start.6
  0.6 0.7 %copy-start.4 = (s32[2,8]{1,0:T(2,128)S(1)}, s32[2,8]{1,0:T(2,128)}, u32[]{:S(2)}) copy-start(s32[2,8]{1,0:T(2,128)} %positions.1) | copy-start | bytes 196
  1.3 0.7 %copy-start.3 = (bf16[64,8]{0,1:T(8,128)(2,1)S(1)}, bf16[64,8]{0,1:T(8,128)(2,1)}, u32[]{:S(2)}) copy-start(bf16[64,8]{0,1:T(8,128)(2,1)} %param.7) | copy-start | bytes 3076
  2.2 26.7 %copy-start.1 = (s32[2,1024]{1,0:T(2,128)S(1)}, s32[2,1024]{1,0:T(2,128)}, u32[]{:S(2)}) copy-start(s32[2,1024]{1,0:T(2,128)} %refs_4_.1) | copy-start | bytes 24580
  2.2 26.7 %copy-start.2 = (f32[2,1024]{1,0:T(2,128)S(1)}, f32[2,1024]{1,0:T(2,128)}, u32[]{:S(2)}) copy-start(f32[2,1024]{1,0:T(2,128)} %refs_5_.1) | copy-start | bytes 24580
  28.3 0.7 copy-start.5
  28.3 2.3 %collective-permute-start.1 = (bf16[512,128]{1,0:T(8,128)(2,1)S(1)}, bf16[512,128]{1,0:T(8,128)(2,1)S(1)}, u32[]{:S(2)}, u32[]{:S(2)}) collective-permute-start(bf16[512,128]{1,0:T(8,128)(2,1)S(1)} %bitcast.6), channel_id=1, source_target_pairs={{0,1},{1,0},{2,3},{3,2},{4,5},{5,4},{6,7},{7,6},{8,9},{9,8},{10,11... | collective-permute-start | bytes 393224 | tf_op jit(solution)/shard_map/ppermute | solution.py:240
  28.3 5.9 %collective-permute-start = (bf16[512,128]{1,0:T(8,128)(2,1)S(1)}, bf16[512,128]{1,0:T(8,128)(2,1)S(1)}, u32[]{:S(2)}, u32[]{:S(2)}) collective-permute-start(bf16[512,128]{1,0:T(8,128)(2,1)S(1)} %bitcast.7), channel_id=1, source_target_pairs={{0,64},{64,0},{1,65},{65,1},{2,66},{66,2},{3,67},{67,3},{4,68},{68... | collective-permute-start | bytes 393224 | tf_op jit(solution)/shard_map/ppermute | solution.py:239
  34.2 1.7 %copy-start = (bf16[1024,128]{1,0:T(8,128)(2,1)S(1)}, bf16[1024,128]{1,0:T(8,128)(2,1)}, u32[]{:S(2)}) copy-start(bf16[1024,128]{1,0:T(8,128)(2,1)} %refs_6_.1) | copy-start | bytes 786436
  34.2 1.6 %collective-permute-start.2 = (bf16[512,128]{1,0:T(8,128)(2,1)S(1)}, bf16[512,128]{1,0:T(8,128)(2,1)S(1)}, u32[]{:S(2)}, u32[]{:S(2)}) collective-permute-start(bf16[512,128]{1,0:T(8,128)(2,1)S(1)} %collective-permute-done.refs_0_), channel_id=1, source_target_pairs={{0,1},{1,0},{2,3},{3,2},{4,5},{5,4},{6,7},{7,6},{8,9},{9,8},{10,11... | collective-permute-start | bytes 393224 | tf_op jit(solution)/shard_map/ppermute | solution.py:265

commit v9 on v8

--- a/solution.py
+++ b/solution.py
@@ -141,17 +141,19 @@
     sums = lax.dot_general(weights[...], res, NT, preferred_element_type=F32)
     fields[0:1, :] = sums[0:1] + sums[1:2] + sums[2:3]
     fields[1:2, :] = sums[3:4] + sums[4:5] + sums[5:6]
-    fields[2:4, :] = cells[...].astype(F32) + 0.5 * fractions[...]
-    fields[4:8, :] = jnp.zeros((4, rows), F32)
+    fields[2:4, :] = cells[...].astype(F32)
+    fields[4:6, :] = jnp.zeros((2, rows), F32)
+    fields[6:8, :] = 0.5 * fractions[...]
     everything = fields[...]
     row_of = lax.broadcasted_iota(jnp.int32, (4, slot), 0)
     place = lax.broadcasted_iota(jnp.int32, (4, slot), 1)
     for t in range(tiles):
-        moved = pltpu.roll(everything, (rows - start[t]) & (rows - 1), 1)[:4, :slot]
-        moved = jnp.where((row_of >= 2) | (place < counts[0, t]), moved, 0.0)
+        turned = pltpu.roll(everything, (rows - start[t]) & (rows - 1), 1)[:, :slot]
+        moved = jnp.where((row_of >= 2) | (place < counts[0, t]), turned[:4], 0.0)
+        halves = turned[4:]
         for owner in range(owners):
             base = float((t * owners + owner) * (GRID // (tiles * owners)))
-            packed[owner, t] = moved - jnp.where(row_of == 2, base, 0.0)
+            packed[owner, t] = (moved - jnp.where(row_of == 2, base, 0.0)) + halves
 
 
 def tap_weights(position, count):
@@ -216,7 +218,7 @@
     owners = lax.axis_size(VIS)
     slot = rows // 2
     width = GRID // tiles
-    plane = ("vis_a", "vis_1", "tile_0")
+    plane = ("vis_1", "vis_a", "tile_0")
     members = lax.axis_size(plane)
     count = spectra.shape[1]
     line = lax.axis_size(LINE)

time: 68.2 us -> 68.3 us (level)
  no operation moved by 1% of the time
where the time goes in v9:
time: 68.3 us; the launch traced here: 67.9 us
  blocking collectives  52.5 us (77%)
  Pallas kernels  10.7 us (16%)
  waiting for transfers between devices  1.96 us (3%)
  local copies, waits for them, and re-layouts  1.43 us (2%)
  between operations  0.74 us (1%)
    all_to_all x1, blocking collectives, on_device(): lax.all_to_all(mine, plane, 0, 0, tiled=True).reshape(members * count, 128)  25.6 us
    all_to_all x1, blocking collectives, on_device(): parts = lax.all_to_all(partial, VIS, 0, 0, tiled=True)  14.6 us
    all_to_all x1, blocking collectives, on_device(): lax.all_to_all(packed.reshape(line * tiles, 4, slot), LINE + TILE, 0, 0,...  12.3 us
    pallas_call x1, Pallas kernels, on_device(): pl.pallas_call(second_kernel, out_shape=(jax.ShapeDtypeStruct(observed.sh...  2.59 us
    pallas_call x1, Pallas kernels, on_device(): pl.pallas_call(grid_kernel, out_shape=(jax.ShapeDtypeStruct((owners, 2 *...  2.4 us
    ppermute x1, waiting for transfers between devices, on_device(): next_to = lax.ppermute(own, 'vis_b', swap)  1.95 us
    pallas_call x1, Pallas kernels, on_device(): cos_sum, sin_sum = middle(other, factors, cos_sum, sin_sum)  1.65 us
    pallas_call x1, Pallas kernels, on_device(): pl.pallas_call(first_kernel, out_shape=(jax.ShapeDtypeStruct((rows, 128),...  1.64 us
  transfers between devices with their start and end apart: 3, of which 1 were waited for; matrix products, arithmetic and copies ran while one was open for 0% of the time, Pallas kernels for 7%

profile of v9, /device:TPU:32, one launch (start us, length us, event | category | flops | bytes accessed | tf_op | source)
XLA Modules:
  0.0 67.9 jit_solution(17211386874381735232)
XLA Ops:
  0.6 0.0 copy-start.6
  0.6 0.0 copy-start.4
  0.6 0.6 copy-done.6
  1.3 0.0 copy-done.4
  1.3 0.0 copy-start.3
  1.3 0.7 %copy-done.3 = bf16[64,8]{0,1:T(8,128)(2,1)S(1)} copy-done((bf16[64,8]{0,1:T(8,128)(2,1)S(1)}, bf16[64,8]{0,1:T(8,128)(2,1)}, u32[]{:S(2)}) %copy-start.3) | copy-done | bytes 1048
  2.0 0.2 components.1
  2.2 0.0 copy-start.1
  2.2 0.0 copy-start.2
  2.2 25.6 %all_to_all.15 = bf16[64,8,128]{2,1,0:T(8,128)(2,1)S(1)} all-to-all(bf16[64,8,128]{2,1,0:T(8,128)(2,1)S(1)} %get-tuple-element.20), channel_id=1, replica_groups=mesh['vis_a'=2,'vis_b'=2,'vis_1'=8,'tile_0'=4,'tile_1'=2] {'vis_1','vis_..., dimensions={0} | all-to-all | bytes 262144 | tf_op jit(solution)/shard_map/all_to_all | solution.py:238
  27.8 0.0 copy-start.5
  27.8 0.0 collective-permute-start.1
  27.8 0.6 collective-permute-start
  28.4 0.0 copy-done.1
  28.4 0.0 copy-done.2
  28.4 0.1 copy-done.5
  28.5 1.6 %predict_first.1 = (bf16[1024,128]{1,0:T(8,128)(2,1)S(1)}, f32[1024,128]{1,0:T(8,128)S(1)}, f32[1024,128]{1,0:T(8,128)S(1)}, bf16[8,128]{1,0:T(8,128)(2,1)S(1)}) custom-call(bf16[512,128]{1,0:T(8,128)(2,1)S(1)} %bitcast.8, s32[2,1024]{1,0:T(2,128)S(1)} %copy-done.1, f32[2,1024]{1,0:T(2,128)S(1)} %copy-done.2, f32[1,64]{1,0:T(1,128)S(1)} %bitcast.11), custom_call_target="tpu_custom_call" | custom-call | tf_op jit(solution)/shard_map/predict_first/pallas_call | solution.py:244
  30.1 0.0 collective-permute-done.1.refs_0_
  30.1 1.6 %predict_middle.2 = (f32[1024,128]{1,0:T(8,128)S(1)}, f32[1024,128]{1,0:T(8,128)S(1)}) custom-call(bf16[512,128]{1,0:T(8,128)(2,1)S(1)} %collective-permute-done.1.refs_0_, bf16[1024,128]{1,0:T(8,128)(2,1)S(1)} %get-tuple-element.21.refs_1_, f32[1024,128]{1,0:T(8,128)S(1)} %get-tuple-element.22.refs_2_, f32[1024,128]{1,0:T(8,128)S(1)} %get-tuple-element.23.refs_3_), custom_call_target="tpu_custom_call" | custom-call | tf_op jit(solution)/shard_map/predict_middle/pallas_call | solution.py:265
  31.8 2.0 %collective-permute-done.refs_0_ = bf16[512,128]{1,0:T(8,128)(2,1)S(1)} collective-permute-done((bf16[512,128]{1,0:T(8,128)(2,1)S(1)}, bf16[512,128]{1,0:T(8,128)(2,1)S(1)}, u32[]{:S(2)}, u32[]{:S(2)}) %collective-permute-start) | collective-permute-done | bytes 131104 | tf_op jit(solution)/shard_map/ppermute | solution.py:241
  33.7 0.0 copy-start
  33.7 0.0 collective-permute-start.2
  33.8 1.6 %predict_middle.3 = (f32[1024,128]{1,0:T(8,128)S(1)}, f32[1024,128]{1,0:T(8,128)S(1)}) custom-call(bf16[512,128]{1,0:T(8,128)(2,1)S(1)} %collective-permute-done.refs_0_, bf16[1024,128]{1,0:T(8,128)(2,1)S(1)} %get-tuple-element.21.refs_1_, f32[1024,128]{1,0:T(8,128)S(1)} %get-tuple-element.27.refs_2_, f32[1024,128]{1,0:T(8,128)S(1)} %get-tuple-element.28.refs_3_), custom_call_target="tpu_custom_call" | custom-call | tf_op jit(solution)/shard_map/predict_middle/pallas_call | solution.py:268
  35.4 0.0 collective-permute-done.2.refs_0_
  35.4 0.0 copy-done
  35.4 2.6 %predict_second.1 = (bf16[1024,128]{1,0:T(8,128)(2,1)S(1)}, f32[4,8,4,512]{3,2,1,0:T(4,128)S(1)}) custom-call(s32[1,8]{1,0:T(1,128)S(1)} %get-tuple-element.19.counts, bf16[512,128]{1,0:T(8,128)(2,1)S(1)} %collective-permute-done.2.refs_0_, bf16[1024,128]{1,0:T(8,128)(2,1)S(1)} %get-tuple-element.21.refs_1_, f32[1024,128]{1,0:T(8,128)S(1)} %get-tuple-element.29.refs_2_, ...), custom_call_target="tpu_custom_call" | custom-call | tf_op jit(solution)/shard_map/predict_second/pallas_call | solution.py:269
  38.0 12.3 %all_to_all.16.got = f32[32,4,512]{2,1,0:T(4,128)S(1)} all-to-all(f32[32,4,512]{2,1,0:T(4,128)S(1)} %bitcast.9), channel_id=1, replica_groups=mesh['vis_a'=2,'vis_b'=2,'vis_1'=8,'tile_0'=4,'tile_1'=2] {'vis_a','vis_..., dimensions={0} | all-to-all | bytes 524288 | tf_op jit(solution)/shard_map/all_to_all | solution.py:284
  50.3 2.4 %gridding.1 = (bf16[32,8,256]{2,1,0:T(8,128)(2,1)S(1)}, bf16[1024,128]{1,0:T(8,128)(2,1)}) custom-call(f32[32,4,512]{2,1,0:T(4,128)S(1)} %all_to_all.16.got, bf16[1024,128]{1,0:T(8,128)(2,1)S(1)} %get-tuple-element.33.near), custom_call_target="tpu_custom_call" | custom-call | tf_op jit(solution)/shard_map/gridding/pallas_call | solution.py:289
  52.7 14.6 %all_to_all.17 = bf16[32,8,256]{2,1,0:T(8,128)(2,1)S(1)} all-to-all(bf16[32,8,256]{2,1,0:T(8,128)(2,1)S(1)} %get-tuple-element.35), channel_id=1, replica_groups=mesh['vis_a'=2,'vis_b'=2,'vis_1'=8,'tile_0'=4,'tile_1'=2] {'vis_a','vis_..., dimensions={0} | all-to-all | bytes 262144 | tf_op jit(solution)/shard_map/all_to_all | solution.py:301
  67.3 0.6 add_shares.1
Async XLA Ops:
  0.6 0.7 copy-start.6
  0.6 0.7 %copy-start.4 = (s32[2,8]{1,0:T(2,128)S(1)}, s32[2,8]{1,0:T(2,128)}, u32[]{:S(2)}) copy-start(s32[2,8]{1,0:T(2,128)} %positions.1) | copy-start | bytes 196
  1.3 0.7 %copy-start.3 = (bf16[64,8]{0,1:T(8,128)(2,1)S(1)}, bf16[64,8]{0,1:T(8,128)(2,1)}, u32[]{:S(2)}) copy-start(bf16[64,8]{0,1:T(8,128)(2,1)} %param.7) | copy-start | bytes 3076
  2.2 26.3 %copy-start.1 = (s32[2,1024]{1,0:T(2,128)S(1)}, s32[2,1024]{1,0:T(2,128)}, u32[]{:S(2)}) copy-start(s32[2,1024]{1,0:T(2,128)} %refs_4_.1) | copy-start | bytes 24580
  2.2 26.3 %copy-start.2 = (f32[2,1024]{1,0:T(2,128)S(1)}, f32[2,1024]{1,0:T(2,128)}, u32[]{:S(2)}) copy-start(f32[2,1024]{1,0:T(2,128)} %refs_5_.1) | copy-start | bytes 24580
  27.8 0.7 copy-start.5
  27.8 2.3 %collective-permute-start.1 = (bf16[512,128]{1,0:T(8,128)(2,1)S(1)}, bf16[512,128]{1,0:T(8,128)(2,1)S(1)}, u32[]{:S(2)}, u32[]{:S(2)}) collective-permute-start(bf16[512,128]{1,0:T(8,128)(2,1)S(1)} %bitcast.6), channel_id=1, source_target_pairs={{0,1},{1,0},{2,3},{3,2},{4,5},{5,4},{6,7},{7,6},{8,9},{9,8},{10,11... | collective-permute-start | bytes 393224 | tf_op jit(solution)/shard_map/ppermute | solution.py:242
  27.8 5.9 %collective-permute-start = (bf16[512,128]{1,0:T(8,128)(2,1)S(1)}, bf16[512,128]{1,0:T(8,128)(2,1)S(1)}, u32[]{:S(2)}, u32[]{:S(2)}) collective-permute-start(bf16[512,128]{1,0:T(8,128)(2,1)S(1)} %bitcast.7), channel_id=1, source_target_pairs={{0,64},{64,0},{1,65},{65,1},{2,66},{66,2},{3,67},{67,3},{4,68},{68... | collective-permute-start | bytes 393224 | tf_op jit(solution)/shard_map/ppermute | solution.py:241
  33.7 1.7 %copy-start = (bf16[1024,128]{1,0:T(8,128)(2,1)S(1)}, bf16[1024,128]{1,0:T(8,128)(2,1)}, u32[]{:S(2)}) copy-start(bf16[1024,128]{1,0:T(8,128)(2,1)} %refs_6_.1) | copy-start | bytes 786436
  33.7 1.6 %collective-permute-start.2 = (bf16[512,128]{1,0:T(8,128)(2,1)S(1)}, bf16[512,128]{1,0:T(8,128)(2,1)S(1)}, u32[]{:S(2)}, u32[]{:S(2)}) collective-permute-start(bf16[512,128]{1,0:T(8,128)(2,1)S(1)} %collective-permute-done.refs_0_), channel_id=1, source_target_pairs={{0,1},{1,0},{2,3},{3,2},{4,5},{5,4},{6,7},{7,6},{8,9},{9,8},{10,11... | collective-permute-start | bytes 393224 | tf_op jit(solution)/shard_map/ppermute | solution.py:267
